TPU v7x, 256 devices: a 4x2x16 block of a 4x16x16 slice. The times are simulated.
256 devices in a mesh: grp: 2 (over y), seq: 128 (over z, x, core).
Axes of the slice: x: 4, y: 2, z: 16, core: 2. Of those that a mesh axis runs over, the one named last changes fastest.
The devices are a block of a 4x16x16 slice.
Arguments:
- history: bfloat16 [65536, 1024], P(('grp', 'seq')), parts along dimension 0, may hold values from -6 to 6
- candidates: bfloat16 [4096, 1024], P(('grp', 'seq')), parts along dimension 0, may hold values from -6 to 6
- lengths: int32 [8], P('grp'), parts along dimension 0, may hold values from 1 to 16384, 32768 in all
- cand_user: int32 [4096], P(('grp', 'seq')), parts along dimension 0, may hold values from 0 to 3
- w_in: bfloat16 [1, 1024, 4096], replicated, may hold values from -0.125 to 0.125
- w_out: bfloat16 [1, 1024, 1024], replicated, may hold values from -0.1875 to 0.1875
Outputs:
- history_out: bfloat16 [65536, 1024], P(('grp', 'seq')), parts along dimension 0
- cand_out: bfloat16 [4096, 1024], P(('grp', 'seq')), parts along dimension 0
There are 2 independent parts, one for each index of `grp`. A program takes and returns all parts, laid end to end along the dimension named above; an argument that names none is the same for every part. Nothing has to cross between parts.
Inputs may be any that keep to these rules, and one draw needn't show every extreme that they name: Each user's history length is at least 1; the lengths sum to 32768, and one of them is exactly 16384.
All inputs are finite; a program needn't handle non-finite values.
Results may differ from a plain program's by a relative error of at most 0.0075.
Values may be sent and summed in bfloat16 or wider, within the bound.
A program may use at most 128 MiB of HBM per device.

v0:
```python
import jax
import jax.numpy as jnp
from jax import lax
from jax.sharding import Mesh
from jax.sharding import PartitionSpec as P

HEADS = 8
WIN = 8
SEQ = ("seq_0", "seq_1", "seq_2")
GRP_SEQ = ("grp", "seq_0", "seq_1", "seq_2")


eps = 1e-06


def passed_along(value, axis, by):
    peers = lax.axis_size(axis)
    pairs = [(i, i + by) for i in range(peers) if 0 <= i + by < peers]
    return lax.ppermute(value, axis, pairs)


def in_order(parts, dim):
    lengths = list(parts.shape[1:])
    lengths[dim] *= parts.shape[0]
    return jnp.moveaxis(parts, 0, dim).reshape(lengths)


def all_blocks(value, axes, sequence):
    parts = value[None]
    for k in sequence:
        parts = lax.all_gather(parts, axes[k], axis=0, tiled=True)
    block = [lax.axis_size(axes[k]) for k in reversed(sequence)]
    parts = parts.reshape(*block, *value.shape)
    turned = sorted(range(len(sequence)), key=lambda place: sequence[len(sequence) - 1 - place])
    return parts.transpose(*turned, *range(len(sequence), parts.ndim)).reshape(-1, *value.shape)


def whole_of(value, axes, sequence, dim):
    return in_order(all_blocks(value, axes, sequence), dim)


def layer_norm(rows):
    centred = rows - jnp.mean(rows, axis=-1, keepdims=True)
    return centred * lax.rsqrt(jnp.mean(centred * centred, axis=-1, keepdims=True) + eps)


def segment_of(positions, ends):
    return jnp.sum((positions[:, None] >= ends[None, :]).astype(jnp.int32), axis=1)


def per_device(history, candidates, lengths, cand_user, w_in, w_out):
    rows = history.shape[0]
    width = history.shape[1]
    heads = HEADS
    head_dim = width // heads
    scale = head_dim ** (-0.5)
    reach = (WIN - 1) * rows
    myself = lax.axis_index(SEQ)
    ends = jnp.cumsum(lengths)
    q_pos = myself * rows + jnp.arange(rows, dtype=jnp.int32)
    q_seg = segment_of(q_pos, ends)
    k_pos = myself * rows - (WIN - 1) * rows + jnp.arange(WIN * rows, dtype=jnp.int32)
    allowed = (k_pos[None, :] >= 0) & (k_pos[None, :] <= q_pos[:, None])
    allowed = allowed & (q_pos[:, None] - k_pos[None, :] < reach)
    allowed = allowed & (segment_of(k_pos, ends)[None, :] == q_seg[:, None])
    x_rows = history
    c_rows = candidates
    normed = layer_norm(x_rows.astype(jnp.float32)).astype(jnp.bfloat16)
    proj = jax.nn.silu(jnp.dot(normed, w_in[0], preferred_element_type=jnp.float32)).astype(
        jnp.bfloat16
    )
    u_all = proj[:, 0:width]
    v_all = proj[:, width : 2 * width]
    q_all = proj[:, 2 * width : 3 * width]
    k_all = proj[:, 3 * width : 4 * width]
    keyval = jnp.stack((k_all, v_all))
    window = keyval
    for section in range(WIN.bit_length() - 1):
        moved = passed_along(window, SEQ, 2**section)
        window = jnp.concatenate([moved, window], axis=1)
    q_heads = q_all.reshape(rows, heads, head_dim)
    k_heads = window[0].reshape(WIN * rows, heads, head_dim)
    v_heads = window[1].reshape(WIN * rows, heads, head_dim)
    scores = (
        jnp.einsum("qhd,khd->hqk", q_heads, k_heads, preferred_element_type=jnp.float32) * scale
    )
    weight = jnp.where(allowed[None], jax.nn.silu(scores), 0.0).astype(jnp.bfloat16)
    attn = jnp.einsum("hqk,khd->qhd", weight, v_heads, preferred_element_type=jnp.float32).reshape(
        rows, width
    )
    y_rows = (layer_norm(attn) * u_all.astype(jnp.float32)).astype(jnp.bfloat16)
    x_rows = (
        x_rows.astype(jnp.float32) + jnp.dot(y_rows, w_out[0], preferred_element_type=jnp.float32)
    ).astype(jnp.bfloat16)
    cnormed = layer_norm(c_rows.astype(jnp.float32)).astype(jnp.bfloat16)
    u_c = jax.nn.silu(
        jnp.dot(cnormed, w_in[0][:, 0:width], preferred_element_type=jnp.float32)
    ).astype(jnp.bfloat16)
    q_c = jax.nn.silu(
        jnp.dot(cnormed, w_in[0][:, 2 * width : 3 * width], preferred_element_type=jnp.float32)
    ).astype(jnp.bfloat16)
    all_queries = whole_of(q_c, SEQ, (0, 1, 2), 0)
    all_users = whole_of(cand_user, SEQ, (0, 1, 2), 0)
    total_cands = all_queries.shape[0]
    owned = all_users[:, None] == q_seg[None, :]
    cq_heads = all_queries.reshape(total_cands, heads, head_dim)
    own_k = k_all.reshape(rows, heads, head_dim)
    own_v = v_all.reshape(rows, heads, head_dim)
    cscores = (
        jnp.einsum("chd,khd->hck", cq_heads, own_k, preferred_element_type=jnp.float32) * scale
    )
    cweight = jnp.where(owned[None], jax.nn.silu(cscores), 0.0).astype(jnp.bfloat16)
    partial_value = jnp.einsum(
        "hck,khd->chd", cweight, own_v, preferred_element_type=jnp.float32
    ).reshape(total_cands, width)
    cattn = lax.psum_scatter(partial_value, SEQ, scatter_dimension=0, tiled=True)
    y_c = (layer_norm(cattn) * u_c.astype(jnp.float32)).astype(jnp.bfloat16)
    c_rows = (
        c_rows.astype(jnp.float32) + jnp.dot(y_c, w_out[0], preferred_element_type=jnp.float32)
    ).astype(jnp.bfloat16)
    return (x_rows, c_rows)


def solution(mesh):
    torus = Mesh(
        mesh.devices.reshape(mesh.shape["grp"], 16, 4, 2), ("grp", "seq_0", "seq_1", "seq_2")
    )
    in_specs = (P(GRP_SEQ, None), P(GRP_SEQ, None), P("grp"), P(GRP_SEQ), P(), P())
    out_specs = (P(GRP_SEQ, None), P(GRP_SEQ, None))
    return jax.shard_map(
        per_device, mesh=torus, in_specs=in_specs, out_specs=out_specs, check_vma=False
    )
```

profile of v0, /device:TPU:40, one launch (start us, length us, event | category | flops | bytes accessed | tf_op | source)
XLA Modules:
  0.0 469.3 jit_solution(17617478358884446746)
XLA Ops:
  7.3 1.1 convert_reduce_fusion.1
  8.3 0.9 fusion.56
  9.3 2.1 multiply_convert_fusion.5
  11.4 53.5 %all-gather.1 = bf16[256,1024]{1,0:T(8,128)(2,1)} all-gather(bf16[16,1024]{1,0:T(8,128)(2,1)S(1)} %multiply_convert_fusion.5), channel_id=3, replica_groups=mesh['grp'=2,'seq_0'=16,'seq_1'=4,'seq_2'=2] {'seq_0'}, dimensions={0}, use_global_device_ids=true | all-gather | bytes 557056 | tf_op jit(solution)/shard_map/all_gather | solution.py:31
  65.0 30.0 %all-gather.6.cloned.1.call-done = bf16[64,16,1024]{2,1,0:T(8,128)(2,1)} async-done(((bf16[16,16,1024]{2,1,0:T(8,128)(2,1)}), bf16[64,16,1024]{2,1,0:T(8,128)(2,1)}) %all-gather.6.cloned.1.call-update) | async-done | bytes 2097168 | tf_op jit(solution)/shard_map/all_gather | solution.py:31
  95.1 0.1 convert_reduce_fusion
  95.3 0.3 fusion.33
  95.6 5.9 %multiply_convert_fusion = bf16[256,4096]{1,0:T(8,128)(2,1)S(1)} fusion(bf16[256,1024]{1,0:T(8,128)(2,1)S(1)} %copy-done.2, f32[256]{0:T(256)S(1)} %add_rsqrt_fusion.1, f32[256]{0:T(256)S(1)} %broadcast_multiply_fusion.1, bf16[1,1024,4096]{2,1,0:T(8,128)(2,1)} %param.10), kind=kOutput, calls=%fused_computation.11 | convolution fusion | flops 2153775104 | bytes 11012096 | tf_op jit(solution)/shard_map/dot_general | solution.py:69
  101.6 1.3 copy-done.3
  102.9 1.4 slice_bitcast_fusion.2
  104.3 1.1 pad_maximum_fusion
  105.3 2.6 collective-permute-start
  107.9 2.1 copy.68
  110.0 0.2 reduce-window.8
  110.2 0.6 dynamic-slice
  111.4 0.2 dynamic-update-slice
  111.7 20.7 %all-reduce = s32[256]{0:T(256)S(1)} all-reduce(s32[256]{0:T(256)S(1)} %dynamic-update-slice), channel_id=2, replica_groups=mesh['grp'=2,'seq_0'=16,'seq_1'=4,'seq_2'=2] {'seq_0'}, use_global_device_ids=true, to_apply=%add | all-reduce | flops 256 | bytes 2048
  132.5 11.9 %all_gather.19 = s32[64,16]{1,0:T(8,128)S(1)} all-gather(s32[16,16]{1,0:T(8,128)S(1)} %reshape.256), channel_id=1, replica_groups=mesh['grp'=2,'seq_0'=16,'seq_1'=4,'seq_2'=2] {'seq_1'}, dimensions={0}, use_global_device_ids=true | all-gather | bytes 5120 | tf_op jit(solution)/shard_map/all_gather | solution.py:31
  144.5 2.0 all-gather.2
  146.5 0.1 reshape.252
  146.6 0.1 copy.60
  146.7 0.1 eq.39
  146.9 0.1 convert_reduce_fusion.3
  147.0 1.2 broadcast_compare_fusion
  148.1 2.6 copy.61
  150.8 3.0 copy.73
  153.8 12.0 %fusion = f32[8,128,2048]{2,1,0:T(8,128)} fusion(bf16[256,8,128]{0,2,1:T(8,128)(2,1)} %bitcast.76, pred[2048,256]{1,0:T(8,128)(4,1)} %broadcast_compare_fusion, bf16[2048,8,128]{2,1,0:T(8,128)(2,1)} %bitcast.73, bf16[32,8,8,128]{3,2,1,0:T(8,128)(2,1)} %get-tuple-element.4), kind=kOutput, calls=%fused_computation.3 | convolution fusion | flops 2176843776 | bytes 14155776 | tf_op jit(solution)/shard_map/hck,khd->chd/dot_general | solution.py:113
  165.7 9.3 %copy.69 = f32[2048,1024]{1,0:T(8,128)} copy(f32[2048,1024]{0,1:T(8,128)} %bitcast.69) | data formatting | bytes 16777216 | tf_op jit(solution)/shard_map/reshape | solution.py:115
  175.1 1.4 maximum_maximum_fusion.2
  176.5 1.7 collective-permute-start.1
  178.2 45.1 %collective-permute-done.1 = bf16[2,512,1024]{2,1,0:T(8,128)(2,1)S(1)} collective-permute-done((bf16[2,512,1024]{2,1,0:T(8,128)(2,1)S(1)}, bf16[2,512,1024]{2,1,0:T(8,128)(2,1)S(1)}, u32[]{:S(2)}, u32[]{:S(2)}) %collective-permute-start.1) | collective-permute-done | bytes 2097184 | tf_op jit(solution)/shard_map/ppermute | solution.py:19
  223.3 5.4 %maximum_maximum_fusion.1 = bf16[2,1024,1024]{2,1,0:T(8,128)(2,1)} fusion(bf16[1,256,1024]{2,1,0:T(8,128)(2,1)S(1)} %get-tuple-element.5, bf16[1,256,1024]{2,1,0:T(8,128)(2,1)S(1)} %get-tuple-element.8, bf16[2,256,1024]{2,1,0:T(8,128)(2,1)} %collective-permute-done, bf16[2,512,1024]{2,1,0:T(8,128)(2,1)S(1)} %collective-permute-done.1), kind=kLoop, calls=%fused_computation.8 | loop fusion | flops 16777216 | bytes 8388608 | tf_op jit(solution)/shard_map/concatenate | solution.py:80
  228.7 8.2 %collective-permute-start.2 = (bf16[2,1024,1024]{2,1,0:T(8,128)(2,1)}, bf16[2,1024,1024]{2,1,0:T(8,128)(2,1)}, u32[]{:S(2)}, u32[]{:S(2)}) collective-permute-start(bf16[2,1024,1024]{2,1,0:T(8,128)(2,1)} %maximum_maximum_fusion.1), channel_id=1, source_target_pairs={{0,4},{1,5},{2,6},{3,7},{4,8},{5,9},{6,10},{7,11},{8,12},{9,13},{1... | collective-permute-start | bytes 12582920 | tf_op jit(solution)/shard_map/ppermute | solution.py:19
  237.0 0.1 convert_reduce_fusion.2
  237.1 1.7 fusion.19
  238.8 97.0 %collective-permute-done.2 = bf16[2,1024,1024]{2,1,0:T(8,128)(2,1)} collective-permute-done((bf16[2,1024,1024]{2,1,0:T(8,128)(2,1)}, bf16[2,1024,1024]{2,1,0:T(8,128)(2,1)}, u32[]{:S(2)}, u32[]{:S(2)}) %collective-permute-start.2) | collective-permute-done | bytes 4194336 | tf_op jit(solution)/shard_map/ppermute | solution.py:19
  335.8 4.4 maximum_maximum_fusion
  340.2 4.0 slice_bitcast_fusion
  344.2 6.5 %copy.66 = bf16[1,2048,1024]{1,2,0:T(8,128)(2,1)} copy(bf16[1,2048,1024]{2,1,0:T(8,128)(2,1)} %get-tuple-element.3) | data formatting | bytes 8388608 | tf_op jit(solution)/shard_map/reshape;squeeze | solution.py:83
  350.7 5.3 %copy.72 = bf16[256,8,8,128]{3,2,1,0:T(8,128)(2,1)} copy(bf16[256,8,8,128]{3,1,2,0:T(8,128)(2,1)} %get-tuple-element.2) | data formatting | bytes 8388608
  355.9 11.7 %fusion.82 = (f32[256]{0:T(256)S(1)}, f32[8,128,256]{2,1,0:T(8,128)S(1)}) fusion(bf16[2048,8,128]{0,2,1:T(8,128)(2,1)} %bitcast.71, pred[256,2048]{1,0:T(8,128)(4,1)} %fusion.19, bf16[2048,8,128]{2,1,0:T(8,128)(2,1)} %bitcast.72, bf16[32,8,8,128]{3,2,1,0:T(8,128)(2,1)} %get-tuple-element.6), kind=kOutput, calls=%fused_computation.90 | convolution fusion | flops 2177105664 | bytes 10486784 | tf_op jit(solution)/shard_map/hqk,khd->qhd/dot_general | solution.py:88
  367.6 1.4 copy.67
  369.0 0.2 fusion.36
  369.2 3.1 fusion.22
  372.3 85.5 %reduce-scatter.2.cloned.1.call-done = f32[16,1024]{1,0:T(8,128)} async-done(((f32[2048,1024]{1,0:T(8,128)}), f32[16,1024]{1,0:T(8,128)}) %reduce-scatter.2.cloned.1.call-update) | async-done | bytes 65552 | tf_op jit(solution)/shard_map/reduce_scatter | solution.py:116
  457.8 1.0 reduce_sum.98
  458.7 1.0 multiply_reduce_fusion
  459.8 2.9 fusion.30
  (37 shorter events, 0.6 us)
Async XLA Ops:
  7.2 362.0 %copy-start = (bf16[1,1024,1024]{2,1,0:T(8,128)(2,1)S(1)}, bf16[1,1024,1024]{2,1,0:T(8,128)(2,1)}, u32[]{:S(2)}) copy-start(bf16[1,1024,1024]{2,1,0:T(8,128)(2,1)} %param.11) | copy-start | bytes 6291460
  7.2 87.9 %copy-start.2 = (bf16[256,1024]{1,0:T(8,128)(2,1)S(1)}, bf16[256,1024]{1,0:T(8,128)(2,1)}, u32[]{:S(2)}) copy-start(bf16[256,1024]{1,0:T(8,128)(2,1)} %param.6) | copy-start | bytes 1572868
  7.2 87.8 %all-gather.6.cloned.1.call-start = ((), (), s32[]{:S(2)}) async-start(), calls=%async_computation.1 | async-start | bytes 2621440 | tf_op jit(solution)/shard_map/all_gather | solution.py:31
  65.0 83.2 %all-gather.8.cloned.1.call-start = ((), (), s32[]{:S(2)}) async-start(), calls=%async_computation.2 | async-start | bytes 6291456 | tf_op jit(solution)/shard_map/all_gather | solution.py:31
  95.1 362.7 %reduce-scatter.2.cloned.1.call-start = ((), (), s32[]{:S(2)}) async-start(), calls=%async_computation.3 | async-start | bytes 8454144 | tf_op jit(solution)/shard_map/reduce_scatter | solution.py:116
  101.5 1.3 copy-start.3
  102.9 7.1 %copy-start.5 = (s32[4]{0:T(128)S(1)}, s32[4]{0:T(128)}, u32[]{:S(2)}) copy-start(s32[4]{0:T(128)} %param.8) | copy-start | bytes 52
  102.9 7.3 %copy-start.7 = (u32[256]{0:T(256)S(1)}, u32[256]{0:T(256)}, u32[]{:S(2)}) copy-start(u32[256]{0:T(256)} %constant.63) | copy-start | bytes 3076
  102.9 8.5 %copy-start.6 = (s32[16]{0:T(128)S(1)}, s32[16]{0:T(128)}, u32[]{:S(2)}) copy-start(s32[16]{0:T(128)} %param.9) | copy-start | bytes 196
  105.3 69.7 %collective-permute-start = (bf16[2,256,1024]{2,1,0:T(8,128)(2,1)}, bf16[2,256,1024]{2,1,0:T(8,128)(2,1)}, u32[]{:S(2)}, u32[]{:S(2)}) collective-permute-start(bf16[2,256,1024]{2,1,0:T(8,128)(2,1)} %pad_maximum_fusion), channel_id=1, source_target_pairs={{0,1},{1,2},{2,3},{3,4},{4,5},{5,6},{6,7},{7,8},{8,9},{9,10},{10,1... | collective-permute-start | bytes 3145736 | tf_op jit(solution)/shard_map/ppermute | solution.py:19
  176.5 46.8 %collective-permute-start.1 = (bf16[2,512,1024]{2,1,0:T(8,128)(2,1)S(1)}, bf16[2,512,1024]{2,1,0:T(8,128)(2,1)S(1)}, u32[]{:S(2)}, u32[]{:S(2)}) collective-permute-start(bf16[2,512,1024]{2,1,0:T(8,128)(2,1)S(1)} %maximum_maximum_fusion.2), channel_id=1, source_target_pairs={{0,2},{1,3},{2,4},{3,5},{4,6},{5,7},{6,8},{7,9},{8,10},{9,11},{10,... | collective-permute-start | bytes 6291464 | tf_op jit(solution)/shard_map/ppermute | solution.py:19
  223.3 5.5 %copy-start.1 = (bf16[2,512,1024]{2,1,0:T(8,128)(2,1)}, bf16[2,512,1024]{2,1,0:T(8,128)(2,1)S(1)}, u32[]{:S(2)}) copy-start(bf16[2,512,1024]{2,1,0:T(8,128)(2,1)S(1)} %collective-permute-done.1) | copy-start | bytes 6291460
  228.7 107.1 %collective-permute-start.2 = (bf16[2,1024,1024]{2,1,0:T(8,128)(2,1)}, bf16[2,1024,1024]{2,1,0:T(8,128)(2,1)}, u32[]{:S(2)}, u32[]{:S(2)}) collective-permute-start(bf16[2,1024,1024]{2,1,0:T(8,128)(2,1)} %maximum_maximum_fusion.1), channel_id=1, source_target_pairs={{0,4},{1,5},{2,6},{3,7},{4,8},{5,9},{6,10},{7,11},{8,12},{9,13},{1... | collective-permute-start | bytes 12582920 | tf_op jit(solution)/shard_map/ppermute | solution.py:19
  367.6 92.2 %copy-start.4 = (bf16[16,1024]{1,0:T(8,128)(2,1)S(1)}, bf16[16,1024]{1,0:T(8,128)(2,1)}, u32[]{:S(2)}) copy-start(bf16[16,1024]{1,0:T(8,128)(2,1)} %param.7) | copy-start | bytes 98308
Sparse Core Ops, SparseCore 0:
  65.1 29.8 all-gather.5
  96.8 22.5 all-gather.7
  175.2 282.5 reduce-scatter.1
where the time goes:
time: 470 us; the launch traced here: 469 us
  waiting for transfers between devices  258 us (55%)
  blocking collectives  88.2 us (19%)
  local copies, waits for them, and re-layouts  38.2 us (8%)
  matrix products  37.7 us (8%)
  other arithmetic  20.2 us (4%)
  between operations  14.6 us (3%)
  starting transfers between devices  12.7 us (3%)
    ppermute x3, waiting for transfers between devices, passed_along(): return lax.ppermute(value, axis, pairs)  142 us
    reduce_scatter x1, waiting for transfers between devices, per_device(): lax.psum_scatter(partial_value, SEQ, scatter_dimension=0, tiled=True)  85.5 us
    all_gather x3, blocking collectives, all_blocks(): parts = lax.all_gather(parts, axes[k], axis=0, tiled=True)  67.5 us
    all_gather x2, waiting for transfers between devices, all_blocks(): parts = lax.all_gather(parts, axes[k], axis=0, tiled=True)  30 us
    unnamed x1, blocking collectives  20.7 us
    unnamed x24, local copies, waits for them, and re-layouts  15.9 us
    ppermute x3, starting transfers between devices, passed_along(): return lax.ppermute(value, axis, pairs)  12.5 us
    dot_general x1, matrix products, per_device(): jnp.einsum('hck,khd->chd', cweight, own_v, preferred_element_type=jnp.flo...  12 us
  transfers between devices with their start and end apart: 6, of which 4 were waited for; matrix products, arithmetic and copies ran while one was open for 18% of the time, Pallas kernels for 0%

commit v1 on v0

v1 whole, which is shorter than its diff:
```python
import functools

import jax
import jax.numpy as jnp
from jax import lax
from jax.experimental import pallas as pl
from jax.experimental.pallas import tpu as pltpu
from jax.sharding import PartitionSpec as P

HEADS = 8
WIN = 8
STAGES = 4
PREV = WIN - 1
SLOTS = 16
OWN = SLOTS - 1
EPS = 1e-06
BIG = 2.0**30
MESH = pl.DeviceIdType.MESH
F32 = jnp.float32
BF16 = jnp.bfloat16


def silu(s):
    h = 0.5 * s
    return h * jnp.tanh(h) + h


def layer_norm(rows):
    centred = rows - jnp.mean(rows, axis=-1, keepdims=True)
    return centred * lax.rsqrt(jnp.mean(centred * centred, axis=-1, keepdims=True) + EPS)


def contract_last(a, b):
    return lax.dot_general(a, b, (((1,), (1,)), ((), ())), preferred_element_type=F32)


def kernel(
    nz,
    lens,
    users,
    cand,
    hist,
    w_in,
    w_out,
    x_out,
    c_out,
    w,
    wo,
    xv,
    nv,
    uv,
    yv,
    snd,
    kbuf,
    vbuf,
    qbuf,
    kext,
    qext,
    qc_s,
    qcz,
    us_s,
    usr,
    part,
    rs_s,
    rs_r,
    at_s,
    at_r,
    cat_s,
    cat_r,
    w_sem,
    wo_sem,
    x_sem,
    kv_ss,
    kv_rs,
    fw_ss,
    fw_rs,
    q_ss,
    q_rs,
    qc_ss,
    qc_rs,
    us_ss,
    us_rs,
    qg_ss,
    qg_rs,
    ug_ss,
    ug_rs,
    rs_ss,
    rs_rs,
    at_ss,
    at_rs,
    cat_ss,
    cat_rs,
):
    rows, width = xv.shape
    n_cand = cand.shape[0]
    head_dim = width // HEADS
    n_users = lens.shape[0]
    blocks = w.shape[0] // 4
    bw = w.shape[2]
    me = lax.axis_index("seq")
    z = me // HEADS
    r = lax.rem(me, HEADS)
    chip = r // 2

    def in_row(h):
        return {"seq": z * HEADS + h}

    def along(step):
        return {"seq": lax.rem(z + step + nz, nz) * HEADS + r}

    def remote(src, dst, ss, rs, to):
        return pltpu.make_async_remote_copy(
            src_ref=src, dst_ref=dst, send_sem=ss, recv_sem=rs, device_id=to, device_id_type=MESH
        )

    x_copy = pltpu.make_async_copy(hist, xv, x_sem)
    x_copy.start()

    def w_copy(m, b):
        i = m * blocks + b
        return pltpu.make_async_copy(
            w_in.at[0, :, pl.ds(m * width + b * bw, bw)], w.at[i], w_sem.at[i]
        )

    for m in (2, 3, 1, 0):
        for b in range(blocks):
            w_copy(m, b).start()
    wo_copy = pltpu.make_async_copy(w_out.at[0], wo, wo_sem)
    wo_copy.start()

    barrier = pltpu.get_barrier_semaphore()
    for d in range(1, HEADS):
        pl.semaphore_signal(
            barrier, inc=1, device_id=in_row(lax.rem(r + d, HEADS)), device_id_type=MESH
        )
    for step in (-2, -1, 1, 2):
        pl.semaphore_signal(barrier, inc=1, device_id=along(step), device_id_type=MESH)

    lane = lax.broadcasted_iota(jnp.int32, (rows, head_dim), 1)
    row_id = lax.broadcasted_iota(jnp.int32, (rows, head_dim), 0)
    total = nz * HEADS * rows

    def ext_body(kk, carry):
        first = lax.rem((z * HEADS - PREV + kk) * rows + total, total)
        pos = first + row_id
        seg = jnp.zeros((rows, head_dim), jnp.int32)
        end = jnp.int32(0)
        for u in range(n_users):
            end = end + lens[u]
            seg = seg + jnp.where(pos >= end, 1, 0)
        mine = lane == seg
        kext[kk] = jnp.where(mine, 0.0, -BIG).astype(BF16)

        @pl.when(kk >= PREV)
        def _():
            qext[jnp.maximum(kk - PREV, 0)] = jnp.where(mine, 1.0, 0.0).astype(BF16)

        return carry

    lax.fori_loop(0, PREV + HEADS, ext_body, 0)

    pl.semaphore_wait(barrier, HEADS - 1 + 4)

    scale = 0.5 * head_dim ** (-0.5)
    cnormed = layer_norm(cand[...].astype(F32)).astype(BF16)
    per = bw // head_dim
    for b in range(blocks):
        w_copy(2, b).wait()
        qc = silu(jnp.dot(cnormed, w[2 * blocks + b], preferred_element_type=F32)) * scale
        for i in range(per):
            qc_s[b * per + i] = qc[:, i * head_dim : (i + 1) * head_dim].astype(BF16)
    lane_row = lax.broadcasted_iota(jnp.int32, (1, head_dim), 1)
    user_row = jnp.zeros((1, head_dim), F32)
    for i in range(n_cand):
        user_row = jnp.where(lane_row == i, users[i].astype(F32), user_row)
    us_s[0] = user_row

    def qc_copy(d):
        h = lax.rem(r + d, HEADS)
        return remote(qc_s.at[h], qcz.at[OWN, r], qc_ss.at[d], qc_rs.at[d], in_row(h))

    def us_copy(d):
        h = lax.rem(r + d, HEADS)
        return remote(us_s.at[0], usr.at[OWN, r], us_ss.at[d], us_rs.at[d], in_row(h))

    def qc_arrival(d):
        j = lax.rem(r - d + HEADS, HEADS)
        return remote(qc_s.at[j], qcz.at[OWN, j], qc_ss.at[d], qc_rs.at[d], in_row(j))

    def us_arrival(d):
        j = lax.rem(r - d + HEADS, HEADS)
        return remote(us_s.at[0], usr.at[OWN, j], us_ss.at[d], us_rs.at[d], in_row(j))

    for d in range(1, HEADS):
        qc_copy(d).start()
        us_copy(d).start()
    qcz[OWN, r] = qc_s[r]
    usr[OWN, r] = us_s[0]

    x_copy.wait()

    def norm_body(i, carry):
        part_rows = pl.ds(pl.multiple_of(i * 64, 64), 64)
        nv[part_rows, :] = layer_norm(xv[part_rows, :].astype(F32)).astype(BF16)
        return carry

    lax.fori_loop(0, rows // 64, norm_body, 0)

    bufs = (kbuf, vbuf, qbuf)

    def row_copy(m, h):
        if m == 2:
            return remote(snd.at[m, h], qbuf.at[r], q_ss.at[h], q_rs.at[r], in_row(h))
        return remote(
            snd.at[m, h], bufs[m].at[PREV + r], kv_ss.at[m, h], kv_rs.at[m, r], in_row(h)
        )

    def row_arrival(m, j):
        if m == 2:
            return remote(snd.at[m, j], qbuf.at[j], q_ss.at[j], q_rs.at[j], in_row(j))
        return remote(
            snd.at[m, j], bufs[m].at[PREV + j], kv_ss.at[m, j], kv_rs.at[m, j], in_row(j)
        )

    def project(m, source):
        if m != 2:
            for b in range(blocks):
                w_copy(source, b).wait()

        def body(i, carry):
            b = lax.rem(chip + i + 1, blocks)
            p = silu(jnp.dot(nv[...], w[source * blocks + b], preferred_element_type=F32))
            if m == 2:
                p = p * scale
            for i2 in range(per):
                h = b * per + i2
                snd[m, h] = p[:, i2 * head_dim : (i2 + 1) * head_dim].astype(BF16)

                @pl.when(h != r)
                def _():
                    row_copy(m, h).start()

            return carry

        lax.fori_loop(0, blocks, body, 0)

    project(0, 3)
    project(1, 1)
    kbuf[PREV + r] = snd[0, r]
    vbuf[PREV + r] = snd[1, r]

    def gather_pairs(stage):
        ahead = OWN if stage == 1 else 2 * stage - 3
        behind = OWN if stage == 1 else 5 + 2 * stage
        pairs = [(ahead, 2 * stage - 1, 2), (ahead, 2 * stage - 2, 1)]
        if stage < STAGES:
            pairs.append((behind, 7 + 2 * stage, -2))
        pairs.append((behind, 6 + 2 * stage, -1))
        return pairs

    def gather_copies(stage):
        for src, dst, step in gather_pairs(stage):
            yield remote(qcz.at[src], qcz.at[dst], qg_ss.at[dst], qg_rs.at[dst], along(step))
            yield remote(usr.at[src], usr.at[dst], ug_ss.at[dst], ug_rs.at[dst], along(step))

    for d in range(1, HEADS):
        qc_arrival(d).wait_recv()
        us_arrival(d).wait_recv()
    for copy in gather_copies(1):
        copy.start()

    project(2, 2)
    qbuf[r] = snd[2, r]

    for b in range(blocks):
        w_copy(0, b).wait()
        u = silu(jnp.dot(nv[...], w[b], preferred_element_type=F32))
        uv[:, b * bw : (b + 1) * bw] = u.astype(BF16)

    def forward(m, j):
        to = jnp.maximum(j - 1, 0)
        return remote(
            bufs[m].at[PREV + j], bufs[m].at[to], fw_ss.at[m, to], fw_rs.at[m, to], along(1)
        )

    def forward_arrival(m, kk):
        return remote(
            bufs[m].at[PREV + kk + 1], bufs[m].at[kk], fw_ss.at[m, kk], fw_rs.at[m, kk], along(1)
        )

    def forward_all(m):
        @pl.when(r >= 1)
        def _():
            forward(m, r).start()

        def body(i, carry):
            d = i + 1
            j = lax.rem(r - d + HEADS, HEADS)
            row_arrival(m, j).wait_recv()

            @pl.when(j >= 1)
            def _():
                forward(m, j).start()

            return carry

        lax.fori_loop(0, HEADS - 1, body, 0)

    def gather_step(stage):
        for copy in gather_copies(stage - 1):
            copy.wait_recv()
        if stage <= STAGES:
            for copy in gather_copies(stage):
                copy.start()

    forward_all(0)
    gather_step(2)
    forward_all(1)
    gather_step(3)

    slot_lane = lax.broadcasted_iota(jnp.int32, (2 * HEADS * n_cand, head_dim), 1)
    slot_row = lax.broadcasted_iota(jnp.int32, (2 * HEADS * n_cand, head_dim), 0)

    def key_block(kk):
        return jnp.concatenate([kbuf[kk], kext[kk]], axis=1)

    def score(g):
        q = qcz[pl.ds(2 * g, 2)].reshape(2 * HEADS * n_cand, head_dim)
        named = jnp.concatenate(
            [
                jnp.broadcast_to(usr[2 * g + a, j], (n_cand, head_dim))
                for a in range(2)
                for j in range(HEADS)
            ],
            axis=0,
        )
        picked = jnp.where(slot_lane == lax.rem(slot_row, n_cand), named, 0.0)
        user = jnp.sum(picked, axis=1, keepdims=True).astype(jnp.int32)
        ext = jnp.where(slot_lane == user, 1.0, 0.0).astype(BF16)
        qx = jnp.concatenate([q, ext], axis=1)
        acc = jnp.zeros((2 * HEADS * n_cand, head_dim), F32)
        for j in range(HEADS):
            h = contract_last(qx, key_block(PREV + j))
            weight = (h * jnp.tanh(h) + h).astype(BF16)
            acc = acc + jnp.dot(weight, vbuf[PREV + j], preferred_element_type=F32)
        part[pl.ds(2 * g, 2)] = acc.reshape(2, HEADS * n_cand, head_dim)

    def rs_copy(i, step):
        return remote(rs_s.at[i], rs_r.at[i], rs_ss.at[i], rs_rs.at[i], along(step))

    def odd_sends(stage):
        k = STAGES - stage
        rs_s[4 + k] = part[2 * stage - 2].astype(BF16)
        rs_copy(4 + k, -1).start()
        rs_s[12 + k] = part[6 + 2 * stage].astype(BF16)
        rs_copy(12 + k, 1).start()

    def score_stage(stage):
        def body(i, carry):
            score(stage - 1 + STAGES * i)
            return carry

        lax.fori_loop(0, 2, body, 0)
        odd_sends(stage)

    score_stage(1)
    gather_step(4)
    score_stage(2)
    score_stage(3)
    gather_step(5)
    score_stage(4)

    def arrived(stage):
        k = stage - 1
        low = rs_r[k].astype(F32) + rs_r[4 + k].astype(F32)
        high = rs_r[12 + k].astype(F32)
        if stage > 1:
            high = high + rs_r[8 + k].astype(F32)
        return low, high

    def rs_wait(stage):
        k = stage - 1
        rs_copy(k, -2).wait_recv()
        rs_copy(4 + k, -1).wait_recv()
        if stage > 1:
            rs_copy(8 + k, 2).wait_recv()
        rs_copy(12 + k, 1).wait_recv()

    def rs_step(stage):
        k = stage - 1
        e = 2 * WIN // 2 + 2 - 2 * stage
        if stage == 1:
            rs_s[k] = part[e - 1].astype(BF16)
        else:
            rs_wait(stage - 1)
            low, high = arrived(stage - 1)
            rs_s[k] = (part[e - 1] + low).astype(BF16)
            rs_s[8 + k] = (part[7 + e] + high).astype(BF16)
            rs_copy(8 + k, 2).start()
        rs_copy(k, -2).start()

    tri_row = lax.broadcasted_iota(jnp.int32, (rows, rows), 0)
    tri_col = lax.broadcasted_iota(jnp.int32, (rows, rows), 1)

    def at_copy(j):
        return remote(at_s.at[j], at_r.at[r], at_ss.at[j], at_rs.at[r], in_row(j))

    def at_arrival(j):
        return remote(at_s.at[j], at_r.at[j], at_ss.at[j], at_rs.at[j], in_row(j))

    def attend(i, carry):
        j = HEADS - 1 - i

        @pl.when(j < PREV)
        def _():
            forward_arrival(0, jnp.minimum(j, PREV - 1)).wait_recv()
            forward_arrival(1, jnp.minimum(j, PREV - 1)).wait_recv()

        @pl.when(j != r)
        def _():
            row_arrival(2, j).wait_recv()

        qx = jnp.concatenate([qbuf[j], qext[j]], axis=1)
        acc = jnp.zeros((rows, head_dim), F32)
        for t in range(WIN):
            h = contract_last(qx, key_block(j + t))
            if t == 0:
                h = jnp.where(tri_col > tri_row, h, -BIG)
            if t == WIN - 1:
                h = jnp.where(tri_col <= tri_row, h, -BIG)
            weight = (h * jnp.tanh(h) + h).astype(BF16)
            acc = acc + jnp.dot(weight, vbuf[j + t], preferred_element_type=F32)
        at_s[j] = acc.astype(BF16)

        @pl.when(j != r)
        def _():
            at_copy(j).start()

        return carry

    rs_step(1)
    lax.fori_loop(0, HEADS // 2, attend, 0)
    rs_step(2)
    lax.fori_loop(HEADS // 2, HEADS, attend, 0)
    at_r[r] = at_s[r]
    rs_step(3)

    def at_wait(i, carry):
        at_arrival(lax.rem(r + i + 1, HEADS)).wait_recv()
        return carry

    lax.fori_loop(0, HEADS - 1, at_wait, 0)

    def y_body(i, carry):
        part_rows = pl.ds(pl.multiple_of(i * 64, 64), 64)
        a = jnp.concatenate([at_r[h, part_rows, :] for h in range(HEADS)], axis=1)
        y = layer_norm(a.astype(F32)) * uv[part_rows, :].astype(F32)
        yv[part_rows, :] = y.astype(BF16)
        return carry

    lax.fori_loop(0, rows // 64, y_body, 0)
    wo_copy.wait()
    for b in range(width // 256):
        cols = slice(b * 256, (b + 1) * 256)
        o = jnp.dot(yv[...], wo[:, cols], preferred_element_type=F32)
        x_out[:, cols] = (xv[:, cols].astype(F32) + o).astype(BF16)

    rs_step(4)
    u_c = jnp.concatenate(
        [
            silu(jnp.dot(cnormed, w[b], preferred_element_type=F32)).astype(BF16)
            for b in range(blocks)
        ],
        axis=1,
    ).astype(F32)
    rs_wait(4)
    low, high = arrived(4)
    cat_s[...] = (part[OWN] + low + high).reshape(HEADS, n_cand, head_dim)

    def cat_copy(d):
        h = lax.rem(r + d, HEADS)
        return remote(cat_s.at[h], cat_r.at[r], cat_ss.at[d], cat_rs.at[d], in_row(h))

    def cat_arrival(d):
        j = lax.rem(r - d + HEADS, HEADS)
        return remote(cat_s.at[j], cat_r.at[j], cat_ss.at[d], cat_rs.at[d], in_row(j))

    for d in range(1, HEADS):
        cat_copy(d).start()
    cat_r[r] = cat_s[r]
    for d in range(1, HEADS):
        cat_arrival(d).wait_recv()
    a = jnp.concatenate([cat_r[h] for h in range(HEADS)], axis=1)
    y_c = (layer_norm(a) * u_c).astype(BF16)
    o = jnp.dot(y_c, wo[...], preferred_element_type=F32)
    c_out[...] = (cand[...].astype(F32) + o).astype(BF16)

    for d in range(1, HEADS):
        qc_copy(d).wait_send()
        us_copy(d).wait_send()
        cat_copy(d).wait_send()
    for stage in range(1, STAGES + 1):
        for copy in gather_copies(stage):
            copy.wait_send()
        k = stage - 1
        rs_copy(k, -2).wait_send()
        rs_copy(4 + k, -1).wait_send()
        if stage > 1:
            rs_copy(8 + k, 2).wait_send()
        rs_copy(12 + k, 1).wait_send()

    def drain(i, carry):
        h = lax.rem(r + i + 1, HEADS)
        for m in range(3):
            row_copy(m, h).wait_send()
        at_copy(h).wait_send()
        forward(0, i + 1).wait_send()
        forward(1, i + 1).wait_send()
        return carry

    lax.fori_loop(0, HEADS - 1, drain, 0)


def per_device(nz, history, candidates, lengths, cand_user, w_in, w_out):
    rows, width = history.shape
    n_cand = candidates.shape[0]
    hd = width // HEADS
    bw = 256
    dma = pltpu.SemaphoreType.DMA
    vmem = pl.BlockSpec(memory_space=pltpu.VMEM)
    smem = pl.BlockSpec(memory_space=pltpu.SMEM)
    hbm = pl.BlockSpec(memory_space=pl.ANY)
    shards = PREV + HEADS
    scratch = [
        pltpu.VMEM((4 * width // bw, width, bw), BF16),
        pltpu.VMEM((width, width), BF16),
        pltpu.VMEM((rows, width), BF16),
        pltpu.VMEM((rows, width), BF16),
        pltpu.VMEM((rows, width), BF16),
        pltpu.VMEM((rows, width), BF16),
        pltpu.VMEM((3, HEADS, rows, hd), BF16),
        pltpu.VMEM((shards, rows, hd), BF16),
        pltpu.VMEM((shards, rows, hd), BF16),
        pltpu.VMEM((HEADS, rows, hd), BF16),
        pltpu.VMEM((shards, rows, hd), BF16),
        pltpu.VMEM((HEADS, rows, hd), BF16),
        pltpu.VMEM((HEADS, n_cand, hd), BF16),
        pltpu.VMEM((SLOTS, HEADS, n_cand, hd), BF16),
        pltpu.VMEM((1, 1, hd), F32),
        pltpu.VMEM((SLOTS, HEADS, 1, hd), F32),
        pltpu.VMEM((SLOTS, HEADS * n_cand, hd), F32),
        pltpu.VMEM((SLOTS, HEADS * n_cand, hd), BF16),
        pltpu.VMEM((SLOTS, HEADS * n_cand, hd), BF16),
        pltpu.VMEM((HEADS, rows, hd), BF16),
        pltpu.VMEM((HEADS, rows, hd), BF16),
        pltpu.VMEM((HEADS, n_cand, hd), F32),
        pltpu.VMEM((HEADS, n_cand, hd), F32),
        dma((4 * width // bw,)),
        dma,
        dma,
        dma((2, HEADS)),
        dma((2, HEADS)),
        dma((2, PREV)),
        dma((2, PREV)),
        dma((HEADS,)),
        dma((HEADS,)),
        dma((HEADS,)),
        dma((HEADS,)),
        dma((HEADS,)),
        dma((HEADS,)),
        dma((SLOTS,)),
        dma((SLOTS,)),
        dma((SLOTS,)),
        dma((SLOTS,)),
        dma((SLOTS,)),
        dma((SLOTS,)),
        dma((HEADS,)),
        dma((HEADS,)),
        dma((HEADS,)),
        dma((HEADS,)),
    ]
    return pl.pallas_call(
        functools.partial(kernel, nz),
        out_shape=(
            jax.ShapeDtypeStruct(history.shape, BF16),
            jax.ShapeDtypeStruct(candidates.shape, BF16),
        ),
        in_specs=[smem, smem, vmem, hbm, hbm, hbm],
        out_specs=(vmem, vmem),
        scratch_shapes=scratch,
        compiler_params=pltpu.CompilerParams(
            collective_id=0, has_side_effects=True, vmem_limit_bytes=60 * 2**20
        ),
    )(lengths, cand_user, candidates, history, w_in, w_out)


def solution(mesh):
    nz = mesh.shape["seq"] // HEADS
    both = ("grp", "seq")
    return jax.shard_map(
        functools.partial(per_device, nz),
        mesh=mesh,
        in_specs=(P(both, None), P(both, None), P("grp"), P(both), P(), P()),
        out_specs=(P(both, None), P(both, None)),
        check_vma=False,
    )
```

time: 470 us -> 97.7 us (0.21)
  waiting for transfers between devices: 258 us -> 0 us
  Pallas kernels: 0 us -> 92.5 us
  blocking collectives: 88.2 us -> 0 us
  matrix products: 37.7 us -> 0 us
  local copies, waits for them, and re-layouts: 38.2 us -> 3.24 us
  other arithmetic: 20.2 us -> 0 us
  between operations: 14.6 us -> 0.64 us
  starting transfers between devices: 12.7 us -> 0 us
    ppermute x3 -> x0, waiting for transfers between devices: 142 us -> none  [passed_along(): return lax.ppermute(value, axis, pairs)]
    pallas_call x0 -> x1, Pallas kernels: none -> 92.5 us  [per_device(): pl.pallas_call(functools.partial(kernel, nz), out_shape=(jax.ShapeDtypeSt...]
    reduce_scatter x1 -> x0, waiting for transfers between devices: 85.5 us -> none  [per_device(): lax.psum_scatter(partial_value, SEQ, scatter_dimension=0, tiled=True)]
    all_gather x3 -> x0, blocking collectives: 67.5 us -> none  [all_blocks(): parts = lax.all_gather(parts, axes[k], axis=0, tiled=True)]
    dot_general x6 -> x0, matrix products: 37.7 us -> none  [the longest x1 12 us: per_device(): jnp.einsum('hck,khd->chd', cweight, own_v, preferred_element_type=jnp.flo...]
    all_gather x2 -> x0, waiting for transfers between devices: 30 us -> none  [all_blocks(): parts = lax.all_gather(parts, axes[k], axis=0, tiled=True)]
    unnamed x1 -> x0, blocking collectives: 20.7 us -> none
    reshape x4 -> x0, local copies, waits for them, and re-layouts: 12.8 us -> none  [the longest x1 9.27 us: per_device(): partial_value = jnp.einsum('hck,khd->chd', cweight, own_v, preferred_elem...]
  transfers between devices with their start and end apart: 6 -> 0, of which waited for: 4 -> 0; matrix products, arithmetic and copies ran while one was open for 18% -> 0% of each run, Pallas kernels for 0% -> 0%
where the time goes in v1:
time: 97.7 us; the launch traced here: 96.4 us
  Pallas kernels  92.5 us (95%)
  local copies, waits for them, and re-layouts  3.24 us (3%)
    pallas_call x1, Pallas kernels, per_device(): pl.pallas_call(functools.partial(kernel, nz), out_shape=(jax.ShapeDtypeSt...  92.5 us
    unnamed x2, local copies, waits for them, and re-layouts  3.24 us

profile of v1, /device:TPU:40, one launch (start us, length us, event | category | flops | bytes accessed | tf_op | source)
XLA Modules:
  0.0 96.4 jit_solution(11535103965682501440)
XLA Ops:
  0.6 92.5 %shard_map.77 = (bf16[256,1024]{1,0:T(8,128)(2,1)}, bf16[16,1024]{1,0:T(8,128)(2,1)}) custom-call(s32[4]{0:T(128)} %lens.1, s32[16]{0:T(128)} %users.1, bf16[16,1024]{1,0:T(8,128)(2,1)} %cand.1, bf16[256,1024]{1,0:T(8,128)(2,1)} %hist.1, bf16[1,1024,4096]{2,1,0:T(8,128)(2,1)} %w_in.1, bf16[1,1024,1024]{2,1,0:T(8,128)(2,1)} %w_out.1), custom_call_target="tpu_custom_call" | custom-call | tf_op jit(solution)/shard_map/pallas_call | solution.py:582
  93.1 1.9 %copy.10 = bf16[256,1024]{1,0:T(8,128)(2,1)} copy(bf16[256,1024]{1,0:T(8,128)(2,1)} %get-tuple-element.4) | data formatting | bytes 1048576
  95.0 1.4 %copy.11 = bf16[16,1024]{1,0:T(8,128)(2,1)} copy(bf16[16,1024]{1,0:T(8,128)(2,1)} %get-tuple-element.5) | data formatting | bytes 65536

commit v2 on v1

--- a/solution.py
+++ b/solution.py
@@ -54,8 +54,10 @@
     kbuf,
     vbuf,
     qbuf,
+    qnbuf,
     kext,
     qext,
+    qnext,
     qc_s,
     qcz,
     us_s,
@@ -65,6 +67,8 @@
     rs_r,
     at_s,
     at_r,
+    an_s,
+    an_r,
     cat_s,
     cat_r,
     w_sem,
@@ -72,10 +76,10 @@
     x_sem,
     kv_ss,
     kv_rs,
-    fw_ss,
-    fw_rs,
     q_ss,
     q_rs,
+    qn_ss,
+    qn_rs,
     qc_ss,
     qc_rs,
     us_ss,
@@ -88,6 +92,8 @@
     rs_rs,
     at_ss,
     at_rs,
+    an_ss,
+    an_rs,
     cat_ss,
     cat_rs,
 ):
@@ -105,8 +111,11 @@
     def in_row(h):
         return {"seq": z * HEADS + h}
 
+    def in_rows(step, h):
+        return {"seq": lax.rem(z + step + nz, nz) * HEADS + h}
+
     def along(step):
-        return {"seq": lax.rem(z + step + nz, nz) * HEADS + r}
+        return in_rows(step, r)
 
     def remote(src, dst, ss, rs, to):
         return pltpu.make_async_remote_copy(
@@ -114,7 +123,6 @@
         )
 
     x_copy = pltpu.make_async_copy(hist, xv, x_sem)
-    x_copy.start()
 
     def w_copy(m, b):
         i = m * blocks + b
@@ -122,44 +130,23 @@
             w_in.at[0, :, pl.ds(m * width + b * bw, bw)], w.at[i], w_sem.at[i]
         )
 
-    for m in (2, 3, 1, 0):
-        for b in range(blocks):
-            w_copy(m, b).start()
+    for b in range(blocks):
+        w_copy(2, b).start()
+    x_copy.start()
     wo_copy = pltpu.make_async_copy(w_out.at[0], wo, wo_sem)
-    wo_copy.start()
 
     barrier = pltpu.get_barrier_semaphore()
     for d in range(1, HEADS):
         pl.semaphore_signal(
             barrier, inc=1, device_id=in_row(lax.rem(r + d, HEADS)), device_id_type=MESH
         )
-    for step in (-2, -1, 1, 2):
+    for step in (-2, 2):
         pl.semaphore_signal(barrier, inc=1, device_id=along(step), device_id_type=MESH)
-
-    lane = lax.broadcasted_iota(jnp.int32, (rows, head_dim), 1)
-    row_id = lax.broadcasted_iota(jnp.int32, (rows, head_dim), 0)
-    total = nz * HEADS * rows
-
-    def ext_body(kk, carry):
-        first = lax.rem((z * HEADS - PREV + kk) * rows + total, total)
-        pos = first + row_id
-        seg = jnp.zeros((rows, head_dim), jnp.int32)
-        end = jnp.int32(0)
-        for u in range(n_users):
-            end = end + lens[u]
-            seg = seg + jnp.where(pos >= end, 1, 0)
-        mine = lane == seg
-        kext[kk] = jnp.where(mine, 0.0, -BIG).astype(BF16)
-
-        @pl.when(kk >= PREV)
-        def _():
-            qext[jnp.maximum(kk - PREV, 0)] = jnp.where(mine, 1.0, 0.0).astype(BF16)
-
-        return carry
-
-    lax.fori_loop(0, PREV + HEADS, ext_body, 0)
-
-    pl.semaphore_wait(barrier, HEADS - 1 + 4)
+    for step in (-1, 1):
+        for h in range(HEADS):
+            pl.semaphore_signal(barrier, inc=1, device_id=in_rows(step, h), device_id_type=MESH)
+
+    pl.semaphore_wait(barrier, HEADS - 1 + 2 + 2 * HEADS)
 
     scale = 0.5 * head_dim ** (-0.5)
     cnormed = layer_norm(cand[...].astype(F32)).astype(BF16)
@@ -169,6 +156,10 @@
         qc = silu(jnp.dot(cnormed, w[2 * blocks + b], preferred_element_type=F32)) * scale
         for i in range(per):
             qc_s[b * per + i] = qc[:, i * head_dim : (i + 1) * head_dim].astype(BF16)
+    for m in (3, 1, 0):
+        for b in range(blocks):
+            w_copy(m, b).start()
+    wo_copy.start()
     lane_row = lax.broadcasted_iota(jnp.int32, (1, head_dim), 1)
     user_row = jnp.zeros((1, head_dim), F32)
     for i in range(n_cand):
@@ -205,21 +196,20 @@
         return carry
 
     lax.fori_loop(0, rows // 64, norm_body, 0)
-
     bufs = (kbuf, vbuf, qbuf)
 
     def row_copy(m, h):
         if m == 2:
             return remote(snd.at[m, h], qbuf.at[r], q_ss.at[h], q_rs.at[r], in_row(h))
         return remote(
-            snd.at[m, h], bufs[m].at[PREV + r], kv_ss.at[m, h], kv_rs.at[m, r], in_row(h)
+            snd.at[m, h], bufs[m].at[r], kv_ss.at[m, h], kv_rs.at[m, r], in_row(h)
         )
 
     def row_arrival(m, j):
         if m == 2:
             return remote(snd.at[m, j], qbuf.at[j], q_ss.at[j], q_rs.at[j], in_row(j))
         return remote(
-            snd.at[m, j], bufs[m].at[PREV + j], kv_ss.at[m, j], kv_rs.at[m, j], in_row(j)
+            snd.at[m, j], bufs[m].at[j], kv_ss.at[m, j], kv_rs.at[m, j], in_row(j)
         )
 
     def project(m, source):
@@ -245,9 +235,7 @@
         lax.fori_loop(0, blocks, body, 0)
 
     project(0, 3)
-    project(1, 1)
-    kbuf[PREV + r] = snd[0, r]
-    vbuf[PREV + r] = snd[1, r]
+    kbuf[r] = snd[0, r]
 
     def gather_pairs(stage):
         ahead = OWN if stage == 1 else 2 * stage - 3
@@ -269,42 +257,44 @@
     for copy in gather_copies(1):
         copy.start()
 
+    project(1, 1)
+    vbuf[r] = snd[1, r]
     project(2, 2)
     qbuf[r] = snd[2, r]
 
-    for b in range(blocks):
-        w_copy(0, b).wait()
-        u = silu(jnp.dot(nv[...], w[b], preferred_element_type=F32))
-        uv[:, b * bw : (b + 1) * bw] = u.astype(BF16)
-
-    def forward(m, j):
-        to = jnp.maximum(j - 1, 0)
-        return remote(
-            bufs[m].at[PREV + j], bufs[m].at[to], fw_ss.at[m, to], fw_rs.at[m, to], along(1)
-        )
-
-    def forward_arrival(m, kk):
-        return remote(
-            bufs[m].at[PREV + kk + 1], bufs[m].at[kk], fw_ss.at[m, kk], fw_rs.at[m, kk], along(1)
-        )
-
-    def forward_all(m):
-        @pl.when(r >= 1)
+    def qn_copy(h):
+        return remote(snd.at[2, h], qnbuf.at[r], qn_ss.at[h], qn_rs.at[r], in_rows(-1, h))
+
+    def qn_arrival(j):
+        return remote(snd.at[2, j], qnbuf.at[j], qn_ss.at[j], qn_rs.at[j], in_rows(1, j))
+
+    def qn_sends(first):
+        @pl.when(r < PREV)
         def _():
-            forward(m, r).start()
-
-        def body(i, carry):
-            d = i + 1
-            j = lax.rem(r - d + HEADS, HEADS)
-            row_arrival(m, j).wait_recv()
-
-            @pl.when(j >= 1)
-            def _():
-                forward(m, j).start()
-
-            return carry
-
-        lax.fori_loop(0, HEADS - 1, body, 0)
+            for i in (first, first + 1):
+                qn_copy(lax.rem(r + i + 1, HEADS)).start()
+
+    lane = lax.broadcasted_iota(jnp.int32, (rows, head_dim), 1)
+    row_id = lax.broadcasted_iota(jnp.int32, (rows, head_dim), 0)
+    total = nz * HEADS * rows
+
+    def owner(j):
+        pos = lax.rem((z * HEADS + j) * rows, total) + row_id
+        seg = jnp.zeros((rows, head_dim), jnp.int32)
+        end = jnp.int32(0)
+        for u in range(n_users):
+            end = end + lens[u]
+            seg = seg + jnp.where(pos >= end, 1, 0)
+        return lane == seg
+
+    def ext_body(j, carry):
+        mine = owner(j)
+        kext[j] = jnp.where(mine, 0.0, -BIG).astype(BF16)
+        qext[j] = jnp.where(mine, 1.0, 0.0).astype(BF16)
+        qnext[j] = jnp.where(owner(HEADS + j), 1.0, 0.0).astype(BF16)
+        return carry
+
+    lax.fori_loop(0, HEADS, ext_body, 0)
 
     def gather_step(stage):
         for copy in gather_copies(stage - 1):
@@ -313,37 +303,51 @@
             for copy in gather_copies(stage):
                 copy.start()
 
-    forward_all(0)
     gather_step(2)
-    forward_all(1)
+    qn_sends(0)
+
+    for b in range(blocks):
+        w_copy(0, b).wait()
+        u = silu(jnp.dot(nv[...], w[b], preferred_element_type=F32))
+        uv[:, b * bw : (b + 1) * bw] = u.astype(BF16)
+
     gather_step(3)
-
-    slot_lane = lax.broadcasted_iota(jnp.int32, (2 * HEADS * n_cand, head_dim), 1)
-    slot_row = lax.broadcasted_iota(jnp.int32, (2 * HEADS * n_cand, head_dim), 0)
-
-    def key_block(kk):
-        return jnp.concatenate([kbuf[kk], kext[kk]], axis=1)
-
-    def score(g):
-        q = qcz[pl.ds(2 * g, 2)].reshape(2 * HEADS * n_cand, head_dim)
+    qn_sends(2)
+
+    def kv_wait(i, carry):
+        j = lax.rem(r + i + 1, HEADS)
+        row_arrival(0, j).wait_recv()
+        row_arrival(1, j).wait_recv()
+        return carry
+
+    lax.fori_loop(0, HEADS - 1, kv_wait, 0)
+
+    n_slot = HEADS * n_cand
+    slot_lane = lax.broadcasted_iota(jnp.int32, (4 * n_slot, head_dim), 1)
+    slot_row = lax.broadcasted_iota(jnp.int32, (4 * n_slot, head_dim), 0)
+
+    def key_block(j):
+        return jnp.concatenate([kbuf[j], kext[j]], axis=1)
+
+    def weigh(h):
+        return (h * jnp.tanh(h) + h).astype(BF16)
+
+    def score(slots):
+        q = jnp.concatenate([qcz[i].reshape(n_slot, head_dim) for i in slots], axis=0)
         named = jnp.concatenate(
-            [
-                jnp.broadcast_to(usr[2 * g + a, j], (n_cand, head_dim))
-                for a in range(2)
-                for j in range(HEADS)
-            ],
+            [jnp.broadcast_to(usr[i, j], (n_cand, head_dim)) for i in slots for j in range(HEADS)],
             axis=0,
         )
         picked = jnp.where(slot_lane == lax.rem(slot_row, n_cand), named, 0.0)
         user = jnp.sum(picked, axis=1, keepdims=True).astype(jnp.int32)
         ext = jnp.where(slot_lane == user, 1.0, 0.0).astype(BF16)
         qx = jnp.concatenate([q, ext], axis=1)
-        acc = jnp.zeros((2 * HEADS * n_cand, head_dim), F32)
+        acc = jnp.zeros((4 * n_slot, head_dim), F32)
         for j in range(HEADS):
-            h = contract_last(qx, key_block(PREV + j))
-            weight = (h * jnp.tanh(h) + h).astype(BF16)
-            acc = acc + jnp.dot(weight, vbuf[PREV + j], preferred_element_type=F32)
-        part[pl.ds(2 * g, 2)] = acc.reshape(2, HEADS * n_cand, head_dim)
+            weight = weigh(contract_last(qx, key_block(j)))
+            acc = acc + jnp.dot(weight, vbuf[j], preferred_element_type=F32)
+        for a, i in enumerate(slots):
+            part[i] = acc[a * n_slot : (a + 1) * n_slot]
 
     def rs_copy(i, step):
         return remote(rs_s.at[i], rs_r.at[i], rs_ss.at[i], rs_rs.at[i], along(step))
@@ -356,16 +360,14 @@
         rs_copy(12 + k, 1).start()
 
     def score_stage(stage):
-        def body(i, carry):
-            score(stage - 1 + STAGES * i)
-            return carry
-
-        lax.fori_loop(0, 2, body, 0)
+        score((2 * stage - 2, 2 * stage - 1, 6 + 2 * stage, 7 + 2 * stage))
         odd_sends(stage)
 
     score_stage(1)
     gather_step(4)
+    qn_sends(4)
     score_stage(2)
+    qn_sends(6)
     score_stage(3)
     gather_step(5)
     score_stage(4)
@@ -399,8 +401,10 @@
             rs_copy(8 + k, 2).start()
         rs_copy(k, -2).start()
 
-    tri_row = lax.broadcasted_iota(jnp.int32, (rows, rows), 0)
-    tri_col = lax.broadcasted_iota(jnp.int32, (rows, rows), 1)
+    one_row = lax.broadcasted_iota(jnp.int32, (rows, rows), 0)
+    one_col = lax.broadcasted_iota(jnp.int32, (rows, rows), 1)
+    two_row = lax.broadcasted_iota(jnp.int32, (2 * rows, rows), 0)
+    two_col = lax.broadcasted_iota(jnp.int32, (2 * rows, rows), 1)
 
     def at_copy(j):
         return remote(at_s.at[j], at_r.at[r], at_ss.at[j], at_rs.at[r], in_row(j))
@@ -408,63 +412,79 @@
     def at_arrival(j):
         return remote(at_s.at[j], at_r.at[j], at_ss.at[j], at_rs.at[j], in_row(j))
 
-    def attend(i, carry):
-        j = HEADS - 1 - i
-
-        @pl.when(j < PREV)
-        def _():
-            forward_arrival(0, jnp.minimum(j, PREV - 1)).wait_recv()
-            forward_arrival(1, jnp.minimum(j, PREV - 1)).wait_recv()
-
-        @pl.when(j != r)
-        def _():
-            row_arrival(2, j).wait_recv()
-
-        qx = jnp.concatenate([qbuf[j], qext[j]], axis=1)
-        acc = jnp.zeros((rows, head_dim), F32)
-        for t in range(WIN):
-            h = contract_last(qx, key_block(j + t))
-            if t == 0:
-                h = jnp.where(tri_col > tri_row, h, -BIG)
-            if t == WIN - 1:
-                h = jnp.where(tri_col <= tri_row, h, -BIG)
-            weight = (h * jnp.tanh(h) + h).astype(BF16)
-            acc = acc + jnp.dot(weight, vbuf[j + t], preferred_element_type=F32)
-        at_s[j] = acc.astype(BF16)
-
-        @pl.when(j != r)
-        def _():
-            at_copy(j).start()
-
-        return carry
+    def an_copy(j):
+        return remote(an_s.at[j], an_r.at[r], an_ss.at[j], an_rs.at[r], in_rows(1, j))
+
+    def an_arrival(h):
+        return remote(an_s.at[0], an_r.at[h], an_ss.at[0], an_rs.at[h], in_rows(-1, h))
+
+    def both(ref, p):
+        return ref[2 * p : 2 * p + 2].reshape(2 * rows, head_dim)
+
+    def values(weight, j):
+        return jnp.dot(weight, vbuf[j], preferred_element_type=F32)
+
+    def attend_own(p):
+        for j in (2 * p, 2 * p + 1):
+
+            @pl.when(j != r)
+            def _():
+                row_arrival(2, j).wait_recv()
+
+        qx = jnp.concatenate([both(qbuf, p), both(qext, p)], axis=1)
+        acc = jnp.zeros((2 * rows, head_dim), F32)
+        for j in range(2 * p + 1):
+            h = contract_last(qx, key_block(j))
+            if j == 2 * p:
+                h = jnp.where((two_row >= rows) | (two_col <= two_row), h, -BIG)
+            if 2 * p + 1 - j == PREV:
+                h = jnp.where((two_row < rows) | (two_col > two_row - rows), h, -BIG)
+            acc = acc + values(weigh(h), j)
+        h = contract_last(qx[rows:], key_block(2 * p + 1))
+        h = jnp.where(one_col <= one_row, h, -BIG)
+        at_s[2 * p] = acc[:rows].astype(BF16)
+        at_s[2 * p + 1] = (acc[rows:] + values(weigh(h), 2 * p + 1)).astype(BF16)
+        for j in (2 * p, 2 * p + 1):
+
+            @pl.when(j != r)
+            def _():
+                at_copy(j).start()
+
+    def attend_next(p):
+        many = 2 * p + 1 < PREV
+        qn_arrival(2 * p).wait_recv()
+        q = jnp.concatenate([qnbuf[2 * p], qnext[2 * p]], axis=1)
+        h = contract_last(q, key_block(2 * p + 1))
+        h = jnp.where(one_col > one_row, h, -BIG)
+        acc = values(weigh(h), 2 * p + 1)
+        if many:
+            qn_arrival(2 * p + 1).wait_recv()
+            qx = jnp.concatenate([both(qnbuf, p), both(qnext, p)], axis=1)
+            more = jnp.zeros((2 * rows, head_dim), F32)
+            for j in range(2 * p + 2, HEADS):
+                h = contract_last(qx, key_block(j))
+                if j == 2 * p + 2:
+                    h = jnp.where((two_row < rows) | (two_col > two_row - rows), h, -BIG)
+                more = more + values(weigh(h), j)
+            acc = acc + more[:rows]
+            an_s[2 * p + 1] = more[rows:].astype(BF16)
+        an_s[2 * p] = acc.astype(BF16)
+        an_copy(2 * p).start()
+        if many:
+            an_copy(2 * p + 1).start()
 
     rs_step(1)
-    lax.fori_loop(0, HEADS // 2, attend, 0)
+    attend_next(0)
+    attend_next(1)
+    attend_own(0)
     rs_step(2)
-    lax.fori_loop(HEADS // 2, HEADS, attend, 0)
+    attend_next(2)
+    attend_next(3)
+    attend_own(1)
+    attend_own(2)
+    rs_step(3)
+    attend_own(3)
     at_r[r] = at_s[r]
-    rs_step(3)
-
-    def at_wait(i, carry):
-        at_arrival(lax.rem(r + i + 1, HEADS)).wait_recv()
-        return carry
-
-    lax.fori_loop(0, HEADS - 1, at_wait, 0)
-
-    def y_body(i, carry):
-        part_rows = pl.ds(pl.multiple_of(i * 64, 64), 64)
-        a = jnp.concatenate([at_r[h, part_rows, :] for h in range(HEADS)], axis=1)
-        y = layer_norm(a.astype(F32)) * uv[part_rows, :].astype(F32)
-        yv[part_rows, :] = y.astype(BF16)
-        return carry
-
-    lax.fori_loop(0, rows // 64, y_body, 0)
-    wo_copy.wait()
-    for b in range(width // 256):
-        cols = slice(b * 256, (b + 1) * 256)
-        o = jnp.dot(yv[...], wo[:, cols], preferred_element_type=F32)
-        x_out[:, cols] = (xv[:, cols].astype(F32) + o).astype(BF16)
-
     rs_step(4)
     u_c = jnp.concatenate(
         [
@@ -473,6 +493,7 @@
         ],
         axis=1,
     ).astype(F32)
+
     rs_wait(4)
     low, high = arrived(4)
     cat_s[...] = (part[OWN] + low + high).reshape(HEADS, n_cand, head_dim)
@@ -488,6 +509,42 @@
     for d in range(1, HEADS):
         cat_copy(d).start()
     cat_r[r] = cat_s[r]
+
+    def at_wait(i, carry):
+        at_arrival(lax.rem(r + i + 1, HEADS)).wait_recv()
+        return carry
+
+    lax.fori_loop(0, HEADS - 1, at_wait, 0)
+
+    @pl.when(r < PREV)
+    def _():
+        for h in range(HEADS):
+            an_arrival(h).wait_recv()
+
+    @pl.when(r == PREV)
+    def _():
+        an_r[...] = jnp.zeros_like(an_r)
+
+    def y_body(i, carry):
+        part_rows = pl.ds(pl.multiple_of(i * 64, 64), 64)
+        a = jnp.concatenate(
+            [
+                at_r[h, part_rows, :].astype(F32) + an_r[h, part_rows, :].astype(F32)
+                for h in range(HEADS)
+            ],
+            axis=1,
+        )
+        y = layer_norm(a) * uv[part_rows, :].astype(F32)
+        yv[part_rows, :] = y.astype(BF16)
+        return carry
+
+    lax.fori_loop(0, rows // 64, y_body, 0)
+    wo_copy.wait()
+    for b in range(width // 256):
+        cols = slice(b * 256, (b + 1) * 256)
+        o = jnp.dot(yv[...], wo[:, cols], preferred_element_type=F32)
+        x_out[:, cols] = (xv[:, cols].astype(F32) + o).astype(BF16)
+
     for d in range(1, HEADS):
         cat_arrival(d).wait_recv()
     a = jnp.concatenate([cat_r[h] for h in range(HEADS)], axis=1)
@@ -514,11 +571,15 @@
         for m in range(3):
             row_copy(m, h).wait_send()
         at_copy(h).wait_send()
-        forward(0, i + 1).wait_send()
-        forward(1, i + 1).wait_send()
+        an_copy(i).wait_send()
         return carry
 
     lax.fori_loop(0, HEADS - 1, drain, 0)
+
+    @pl.when(r < PREV)
+    def _():
+        for h in range(HEADS):
+            qn_copy(h).wait_send()
 
 
 def per_device(nz, history, candidates, lengths, cand_user, w_in, w_out):
@@ -530,7 +591,6 @@
     vmem = pl.BlockSpec(memory_space=pltpu.VMEM)
     smem = pl.BlockSpec(memory_space=pltpu.SMEM)
     hbm = pl.BlockSpec(memory_space=pl.ANY)
-    shards = PREV + HEADS
     scratch = [
         pltpu.VMEM((4 * width // bw, width, bw), BF16),
         pltpu.VMEM((width, width), BF16),
@@ -539,10 +599,12 @@
         pltpu.VMEM((rows, width), BF16),
         pltpu.VMEM((rows, width), BF16),
         pltpu.VMEM((3, HEADS, rows, hd), BF16),
-        pltpu.VMEM((shards, rows, hd), BF16),
-        pltpu.VMEM((shards, rows, hd), BF16),
-        pltpu.VMEM((HEADS, rows, hd), BF16),
-        pltpu.VMEM((shards, rows, hd), BF16),
+        pltpu.VMEM((HEADS, rows, hd), BF16),
+        pltpu.VMEM((HEADS, rows, hd), BF16),
+        pltpu.VMEM((HEADS, rows, hd), BF16),
+        pltpu.VMEM((HEADS, rows, hd), BF16),
+        pltpu.VMEM((HEADS, rows, hd), BF16),
+        pltpu.VMEM((HEADS, rows, hd), BF16),
         pltpu.VMEM((HEADS, rows, hd), BF16),
         pltpu.VMEM((HEADS, n_cand, hd), BF16),
         pltpu.VMEM((SLOTS, HEADS, n_cand, hd), BF16),
@@ -553,6 +615,8 @@
         pltpu.VMEM((SLOTS, HEADS * n_cand, hd), BF16),
         pltpu.VMEM((HEADS, rows, hd), BF16),
         pltpu.VMEM((HEADS, rows, hd), BF16),
+        pltpu.VMEM((HEADS, rows, hd), BF16),
+        pltpu.VMEM((HEADS, rows, hd), BF16),
         pltpu.VMEM((HEADS, n_cand, hd), F32),
         pltpu.VMEM((HEADS, n_cand, hd), F32),
         dma((4 * width // bw,)),
@@ -560,8 +624,8 @@
         dma,
         dma((2, HEADS)),
         dma((2, HEADS)),
-        dma((2, PREV)),
-        dma((2, PREV)),
+        dma((HEADS,)),
+        dma((HEADS,)),
         dma((HEADS,)),
         dma((HEADS,)),
         dma((HEADS,)),
@@ -574,6 +638,8 @@
         dma((SLOTS,)),
         dma((SLOTS,)),
         dma((SLOTS,)),
+        dma((HEADS,)),
+        dma((HEADS,)),
         dma((HEADS,)),
         dma((HEADS,)),
         dma((HEADS,)),

time: 97.7 us -> 89.1 us (0.912)
  Pallas kernels: 92.5 us -> 84.2 us
    pallas_call x1, Pallas kernels: 92.5 us -> 84.2 us  [per_device(): pl.pallas_call(functools.partial(kernel, nz), out_shape=(jax.ShapeDtypeSt...]
where the time goes in v2:
time: 89.1 us; the launch traced here: 88.1 us
  Pallas kernels  84.2 us (95%)
  local copies, waits for them, and re-layouts  3.24 us (4%)
    pallas_call x1, Pallas kernels, per_device(): pl.pallas_call(functools.partial(kernel, nz), out_shape=(jax.ShapeDtypeSt...  84.2 us
    unnamed x2, local copies, waits for them, and re-layouts  3.24 us

profile of v2, /device:TPU:40, one launch (start us, length us, event | category | flops | bytes accessed | tf_op | source)
XLA Modules:
  0.0 88.1 jit_solution(17042113976311073000)
XLA Ops:
  0.6 84.2 %shard_map.77 = (bf16[256,1024]{1,0:T(8,128)(2,1)}, bf16[16,1024]{1,0:T(8,128)(2,1)}) custom-call(s32[4]{0:T(128)} %lens.1, s32[16]{0:T(128)} %users.1, bf16[16,1024]{1,0:T(8,128)(2,1)} %cand.1, bf16[256,1024]{1,0:T(8,128)(2,1)} %hist.1, bf16[1,1024,4096]{2,1,0:T(8,128)(2,1)} %w_in.1, bf16[1,1024,1024]{2,1,0:T(8,128)(2,1)} %w_out.1), custom_call_target="tpu_custom_call" | custom-call | tf_op jit(solution)/shard_map/pallas_call | solution.py:648
  84.8 1.9 %copy.10 = bf16[256,1024]{1,0:T(8,128)(2,1)} copy(bf16[256,1024]{1,0:T(8,128)(2,1)} %get-tuple-element.4) | data formatting | bytes 1048576
  86.7 1.4 %copy.11 = bf16[16,1024]{1,0:T(8,128)(2,1)} copy(bf16[16,1024]{1,0:T(8,128)(2,1)} %get-tuple-element.5) | data formatting | bytes 65536

commit v3 on v2

--- a/solution.py
+++ b/solution.py
@@ -36,14 +36,17 @@
 
 def kernel(
     nz,
-    lens,
-    users,
-    cand,
+    lens_in,
+    users_in,
+    cand_in,
     hist,
     w_in,
     w_out,
     x_out,
     c_out,
+    lens,
+    users,
+    cand,
     w,
     wo,
     xv,
@@ -62,6 +65,7 @@
     qcz,
     us_s,
     usr,
+    qce,
     part,
     rs_s,
     rs_r,
@@ -71,6 +75,7 @@
     an_r,
     cat_s,
     cat_r,
+    small_sem,
     w_sem,
     wo_sem,
     x_sem,
@@ -122,13 +127,22 @@
             src_ref=src, dst_ref=dst, send_sem=ss, recv_sem=rs, device_id=to, device_id_type=MESH
         )
 
+    small = [
+        pltpu.make_async_copy(src, dst, small_sem.at[i])
+        for i, (src, dst) in enumerate(((cand_in, cand), (users_in, users), (lens_in, lens)))
+    ]
+    for copy in small:
+        copy.start()
     x_copy = pltpu.make_async_copy(hist, xv, x_sem)
 
     def w_copy(m, b):
         i = m * blocks + b
         return pltpu.make_async_copy(
-            w_in.at[0, :, pl.ds(m * width + b * bw, bw)], w.at[i], w_sem.at[i]
+            w_in.at[0, :, pl.ds(pl.multiple_of(m * width + b * bw, bw), bw)], w.at[i], w_sem.at[i]
         )
+
+    def block_at(i):
+        return lax.rem(chip + i + (i // 2) * (1 - 2 * (i % 2)), blocks)
 
     for b in range(blocks):
         w_copy(2, b).start()
@@ -147,8 +161,13 @@
             pl.semaphore_signal(barrier, inc=1, device_id=in_rows(step, h), device_id_type=MESH)
 
     pl.semaphore_wait(barrier, HEADS - 1 + 2 + 2 * HEADS)
+    for i in range(blocks):
+        w_copy(3, block_at(i)).start()
+        w_copy(1, block_at(i)).start()
 
     scale = 0.5 * head_dim ** (-0.5)
+    for copy in small:
+        copy.wait()
     cnormed = layer_norm(cand[...].astype(F32)).astype(BF16)
     per = bw // head_dim
     for b in range(blocks):
@@ -156,15 +175,15 @@
         qc = silu(jnp.dot(cnormed, w[2 * blocks + b], preferred_element_type=F32)) * scale
         for i in range(per):
             qc_s[b * per + i] = qc[:, i * head_dim : (i + 1) * head_dim].astype(BF16)
-    for m in (3, 1, 0):
-        for b in range(blocks):
-            w_copy(m, b).start()
-    wo_copy.start()
     lane_row = lax.broadcasted_iota(jnp.int32, (1, head_dim), 1)
     user_row = jnp.zeros((1, head_dim), F32)
     for i in range(n_cand):
         user_row = jnp.where(lane_row == i, users[i].astype(F32), user_row)
     us_s[0] = user_row
+
+    for b in range(blocks):
+        w_copy(0, b).start()
+    wo_copy.start()
 
     def qc_copy(d):
         h = lax.rem(r + d, HEADS)
@@ -212,30 +231,28 @@
             snd.at[m, j], bufs[m].at[j], kv_ss.at[m, j], kv_rs.at[m, j], in_row(j)
         )
 
-    def project(m, source):
-        if m != 2:
-            for b in range(blocks):
-                w_copy(source, b).wait()
-
+    def project(mats, first, last):
         def body(i, carry):
-            b = lax.rem(chip + i + 1, blocks)
-            p = silu(jnp.dot(nv[...], w[source * blocks + b], preferred_element_type=F32))
-            if m == 2:
-                p = p * scale
-            for i2 in range(per):
-                h = b * per + i2
-                snd[m, h] = p[:, i2 * head_dim : (i2 + 1) * head_dim].astype(BF16)
-
-                @pl.when(h != r)
-                def _():
-                    row_copy(m, h).start()
+            b = block_at(i)
+            for m, source in mats:
+                if m != 2:
+                    w_copy(source, b).wait()
+                p = silu(jnp.dot(nv[...], w[source * blocks + b], preferred_element_type=F32))
+                if m == 2:
+                    p = p * scale
+                for i2 in range(per):
+                    h = b * per + i2
+                    snd[m, h] = p[:, i2 * head_dim : (i2 + 1) * head_dim].astype(BF16)
+
+                    @pl.when(h != r)
+                    def _():
+                        row_copy(m, h).start()
 
             return carry
 
-        lax.fori_loop(0, blocks, body, 0)
-
-    project(0, 3)
-    kbuf[r] = snd[0, r]
+        lax.fori_loop(first, last, body, 0)
+
+    project(((0, 3), (1, 1)), 0, 2)
 
     def gather_pairs(stage):
         ahead = OWN if stage == 1 else 2 * stage - 3
@@ -257,9 +274,10 @@
     for copy in gather_copies(1):
         copy.start()
 
-    project(1, 1)
+    project(((0, 3), (1, 1)), 2, blocks)
+    kbuf[r] = snd[0, r]
     vbuf[r] = snd[1, r]
-    project(2, 2)
+    project(((2, 2),), 0, blocks)
     qbuf[r] = snd[2, r]
 
     def qn_copy(h):
@@ -303,28 +321,9 @@
             for copy in gather_copies(stage):
                 copy.start()
 
-    gather_step(2)
-    qn_sends(0)
-
-    for b in range(blocks):
-        w_copy(0, b).wait()
-        u = silu(jnp.dot(nv[...], w[b], preferred_element_type=F32))
-        uv[:, b * bw : (b + 1) * bw] = u.astype(BF16)
-
-    gather_step(3)
-    qn_sends(2)
-
-    def kv_wait(i, carry):
-        j = lax.rem(r + i + 1, HEADS)
-        row_arrival(0, j).wait_recv()
-        row_arrival(1, j).wait_recv()
-        return carry
-
-    lax.fori_loop(0, HEADS - 1, kv_wait, 0)
-
     n_slot = HEADS * n_cand
-    slot_lane = lax.broadcasted_iota(jnp.int32, (4 * n_slot, head_dim), 1)
-    slot_row = lax.broadcasted_iota(jnp.int32, (4 * n_slot, head_dim), 0)
+    slot_lane = lax.broadcasted_iota(jnp.int32, (n_slot, head_dim), 1)
+    slot_row = lax.broadcasted_iota(jnp.int32, (n_slot, head_dim), 0)
 
     def key_block(j):
         return jnp.concatenate([kbuf[j], kext[j]], axis=1)
@@ -332,22 +331,46 @@
     def weigh(h):
         return (h * jnp.tanh(h) + h).astype(BF16)
 
-    def score(slots):
+    def name_users(slots):
+        for i in slots:
+            named = jnp.concatenate(
+                [jnp.broadcast_to(usr[i, j], (n_cand, head_dim)) for j in range(HEADS)], axis=0
+            )
+            picked = jnp.where(slot_lane == lax.rem(slot_row, n_cand), named, 0.0)
+            user = jnp.sum(picked, axis=1, keepdims=True).astype(jnp.int32)
+            qce[i] = jnp.where(slot_lane == user, 1.0, 0.0).astype(BF16)
+
+    def chips_shards(*offsets):
+        return [lax.rem(2 * (chip + o) + b, HEADS) for o in offsets for b in range(2)]
+
+    near = chips_shards(0, 1, 3)
+    far = chips_shards(2)
+
+    def kv_wait(shards):
+        for j in shards:
+
+            @pl.when(j != r)
+            def _():
+                row_arrival(0, j).wait_recv()
+                row_arrival(1, j).wait_recv()
+
+    def score(slots, shards, fresh):
         q = jnp.concatenate([qcz[i].reshape(n_slot, head_dim) for i in slots], axis=0)
-        named = jnp.concatenate(
-            [jnp.broadcast_to(usr[i, j], (n_cand, head_dim)) for i in slots for j in range(HEADS)],
-            axis=0,
-        )
-        picked = jnp.where(slot_lane == lax.rem(slot_row, n_cand), named, 0.0)
-        user = jnp.sum(picked, axis=1, keepdims=True).astype(jnp.int32)
-        ext = jnp.where(slot_lane == user, 1.0, 0.0).astype(BF16)
+        ext = jnp.concatenate([qce[i] for i in slots], axis=0)
         qx = jnp.concatenate([q, ext], axis=1)
-        acc = jnp.zeros((4 * n_slot, head_dim), F32)
-        for j in range(HEADS):
+        if fresh:
+            acc = jnp.zeros((len(slots) * n_slot, head_dim), F32)
+        else:
+            acc = jnp.concatenate([part[i] for i in slots], axis=0)
+        for j in shards:
             weight = weigh(contract_last(qx, key_block(j)))
             acc = acc + jnp.dot(weight, vbuf[j], preferred_element_type=F32)
         for a, i in enumerate(slots):
             part[i] = acc[a * n_slot : (a + 1) * n_slot]
+
+    stage_slots = [(2 * k, 2 * k + 1, 8 + 2 * k, 9 + 2 * k) for k in range(STAGES)]
+    stage_slots[0] += (OWN,)
+    stage_slots[STAGES - 1] = stage_slots[STAGES - 1][:-1]
 
     def rs_copy(i, step):
         return remote(rs_s.at[i], rs_r.at[i], rs_ss.at[i], rs_rs.at[i], along(step))
@@ -359,18 +382,34 @@
         rs_s[12 + k] = part[6 + 2 * stage].astype(BF16)
         rs_copy(12 + k, 1).start()
 
-    def score_stage(stage):
-        score((2 * stage - 2, 2 * stage - 1, 6 + 2 * stage, 7 + 2 * stage))
-        odd_sends(stage)
-
-    score_stage(1)
+    gather_step(2)
+    qn_sends(0)
+    for b in range(blocks):
+        w_copy(0, b).wait()
+        u = silu(jnp.dot(nv[...], w[b], preferred_element_type=F32))
+        uv[:, b * bw : (b + 1) * bw] = u.astype(BF16)
+    name_users(stage_slots[0])
+    gather_step(3)
+    qn_sends(2)
+    kv_wait(near)
+    score(stage_slots[0], near, True)
+    name_users(stage_slots[1])
+    score(stage_slots[1], near, True)
     gather_step(4)
     qn_sends(4)
-    score_stage(2)
+    kv_wait(far)
+    score(stage_slots[0], far, False)
+    odd_sends(1)
+    score(stage_slots[1], far, False)
+    odd_sends(2)
+    name_users(stage_slots[2])
+    score(stage_slots[2], near + far, True)
+    odd_sends(3)
     qn_sends(6)
-    score_stage(3)
     gather_step(5)
-    score_stage(4)
+    name_users(stage_slots[3])
+    score(stage_slots[3], near + far, True)
+    odd_sends(4)
 
     def arrived(stage):
         k = stage - 1
@@ -469,23 +508,27 @@
             acc = acc + more[:rows]
             an_s[2 * p + 1] = more[rows:].astype(BF16)
         an_s[2 * p] = acc.astype(BF16)
-        an_copy(2 * p).start()
-        if many:
-            an_copy(2 * p + 1).start()
 
     rs_step(1)
+    attend_own(0)
+    attend_own(1)
+    attend_own(2)
+    rs_step(2)
     attend_next(0)
+    an_copy(0).start()
+    an_copy(1).start()
     attend_next(1)
-    attend_own(0)
-    rs_step(2)
+    an_copy(2).start()
     attend_next(2)
     attend_next(3)
-    attend_own(1)
-    attend_own(2)
     rs_step(3)
+    an_copy(3).start()
+    an_copy(4).start()
+    an_copy(5).start()
     attend_own(3)
     at_r[r] = at_s[r]
     rs_step(4)
+    an_copy(6).start()
     u_c = jnp.concatenate(
         [
             silu(jnp.dot(cnormed, w[b], preferred_element_type=F32)).astype(BF16)
@@ -589,9 +632,11 @@
     bw = 256
     dma = pltpu.SemaphoreType.DMA
     vmem = pl.BlockSpec(memory_space=pltpu.VMEM)
-    smem = pl.BlockSpec(memory_space=pltpu.SMEM)
     hbm = pl.BlockSpec(memory_space=pl.ANY)
     scratch = [
+        pltpu.SMEM(lengths.shape, jnp.int32),
+        pltpu.SMEM(cand_user.shape, jnp.int32),
+        pltpu.VMEM(candidates.shape, BF16),
         pltpu.VMEM((4 * width // bw, width, bw), BF16),
         pltpu.VMEM((width, width), BF16),
         pltpu.VMEM((rows, width), BF16),
@@ -610,6 +655,7 @@
         pltpu.VMEM((SLOTS, HEADS, n_cand, hd), BF16),
         pltpu.VMEM((1, 1, hd), F32),
         pltpu.VMEM((SLOTS, HEADS, 1, hd), F32),
+        pltpu.VMEM((SLOTS, HEADS * n_cand, hd), BF16),
         pltpu.VMEM((SLOTS, HEADS * n_cand, hd), F32),
         pltpu.VMEM((SLOTS, HEADS * n_cand, hd), BF16),
         pltpu.VMEM((SLOTS, HEADS * n_cand, hd), BF16),
@@ -619,6 +665,7 @@
         pltpu.VMEM((HEADS, rows, hd), BF16),
         pltpu.VMEM((HEADS, n_cand, hd), F32),
         pltpu.VMEM((HEADS, n_cand, hd), F32),
+        dma((3,)),
         dma((4 * width // bw,)),
         dma,
         dma,
@@ -647,11 +694,8 @@
     ]
     return pl.pallas_call(
         functools.partial(kernel, nz),
-        out_shape=(
-            jax.ShapeDtypeStruct(history.shape, BF16),
-            jax.ShapeDtypeStruct(candidates.shape, BF16),
-        ),
-        in_specs=[smem, smem, vmem, hbm, hbm, hbm],
+        out_shape=(pltpu.VMEM(history.shape, BF16), pltpu.VMEM(candidates.shape, BF16)),
+        in_specs=[hbm] * 6,
         out_specs=(vmem, vmem),
         scratch_shapes=scratch,
         compiler_params=pltpu.CompilerParams(

time: 89.1 us -> 83.9 us (0.942)
  Pallas kernels: 84.2 us -> 80.5 us
  local copies, waits for them, and re-layouts: 3.24 us -> 1.41 us
    pallas_call x1, Pallas kernels: 84.2 us -> 80.5 us  [per_device(): pl.pallas_call(functools.partial(kernel, nz), out_shape=(pltpu.VMEM(histo...]
    unnamed x2, local copies, waits for them, and re-layouts: 3.24 us -> 1.41 us
where the time goes in v3:
time: 83.9 us; the launch traced here: 82.5 us
  Pallas kernels  80.5 us (96%)
  local copies, waits for them, and re-layouts  1.41 us (2%)
    pallas_call x1, Pallas kernels, per_device(): pl.pallas_call(functools.partial(kernel, nz), out_shape=(pltpu.VMEM(histo...  80.5 us

profile of v3, /device:TPU:40, one launch (start us, length us, event | category | flops | bytes accessed | tf_op | source)
XLA Modules:
  0.0 82.5 jit_solution(8562128337401877144)
XLA Ops:
  0.6 80.5 %shard_map.77 = (bf16[256,1024]{1,0:T(8,128)(2,1)S(1)}, bf16[16,1024]{1,0:T(8,128)(2,1)S(1)}) custom-call(s32[4]{0:T(128)} %lens_in.1, s32[16]{0:T(128)} %users_in.1, bf16[16,1024]{1,0:T(8,128)(2,1)} %cand_in.1, bf16[256,1024]{1,0:T(8,128)(2,1)} %hist.1, bf16[1,1024,4096]{2,1,0:T(8,128)(2,1)} %w_in.1, bf16[1,1024,1024]{2,1,0:T(8,128)(2,1)} %w_out.1), custom_call_target="tpu_custom_call" | custom-call | tf_op jit(solution)/shard_map/pallas_call | solution.py:695
  81.1 0.8 copy.10
  81.9 0.6 copy.11

commit v4 on v3

--- a/solution.py
+++ b/solution.py
@@ -9,11 +9,27 @@
 
 HEADS = 8
 WIN = 8
-STAGES = 4
 PREV = WIN - 1
 SLOTS = 16
 OWN = SLOTS - 1
 EPS = 1e-06
+HOPS = {
+    0: (15, 1),
+    1: (2, -1),
+    2: (15, 3),
+    3: (2, 1),
+    4: (5, -1),
+    5: (15, 6),
+    6: (5, 1),
+    7: (5, 2),
+    8: (15, -1),
+    9: (10, 1),
+    10: (15, -3),
+    11: (10, -1),
+    12: (13, 1),
+    13: (15, -6),
+    14: (13, -1),
+}
 BIG = 2.0**30
 MESH = pl.DeviceIdType.MESH
 F32 = jnp.float32
@@ -154,13 +170,13 @@
         pl.semaphore_signal(
             barrier, inc=1, device_id=in_row(lax.rem(r + d, HEADS)), device_id_type=MESH
         )
-    for step in (-2, 2):
+    for step in (-6, -3, -2, 2, 3, 6):
         pl.semaphore_signal(barrier, inc=1, device_id=along(step), device_id_type=MESH)
     for step in (-1, 1):
         for h in range(HEADS):
             pl.semaphore_signal(barrier, inc=1, device_id=in_rows(step, h), device_id_type=MESH)
 
-    pl.semaphore_wait(barrier, HEADS - 1 + 2 + 2 * HEADS)
+    pl.semaphore_wait(barrier, HEADS - 1 + 6 + 2 * HEADS)
     for i in range(blocks):
         w_copy(3, block_at(i)).start()
         w_copy(1, block_at(i)).start()
@@ -254,25 +270,26 @@
 
     project(((0, 3), (1, 1)), 0, 2)
 
-    def gather_pairs(stage):
-        ahead = OWN if stage == 1 else 2 * stage - 3
-        behind = OWN if stage == 1 else 5 + 2 * stage
-        pairs = [(ahead, 2 * stage - 1, 2), (ahead, 2 * stage - 2, 1)]
-        if stage < STAGES:
-            pairs.append((behind, 7 + 2 * stage, -2))
-        pairs.append((behind, 6 + 2 * stage, -1))
-        return pairs
-
-    def gather_copies(stage):
-        for src, dst, step in gather_pairs(stage):
-            yield remote(qcz.at[src], qcz.at[dst], qg_ss.at[dst], qg_rs.at[dst], along(step))
-            yield remote(usr.at[src], usr.at[dst], ug_ss.at[dst], ug_rs.at[dst], along(step))
+    def gather_copies(slots):
+        copies = []
+        for dst in slots:
+            src, step = HOPS[dst]
+            for ref, ss, rs in ((qcz, qg_ss, qg_rs), (usr, ug_ss, ug_rs)):
+                copies.append(remote(ref.at[src], ref.at[dst], ss.at[dst], rs.at[dst], along(step)))
+        return copies
+
+    def gather_start(*slots):
+        for copy in gather_copies(slots):
+            copy.start()
+
+    def gather_wait(*slots):
+        for copy in gather_copies(slots):
+            copy.wait_recv()
 
     for d in range(1, HEADS):
         qc_arrival(d).wait_recv()
         us_arrival(d).wait_recv()
-    for copy in gather_copies(1):
-        copy.start()
+    gather_start(5, 13, 2, 10, 0, 8)
 
     project(((0, 3), (1, 1)), 2, blocks)
     kbuf[r] = snd[0, r]
@@ -291,6 +308,8 @@
         def _():
             for i in (first, first + 1):
                 qn_copy(lax.rem(r + i + 1, HEADS)).start()
+
+    qn_sends(0)
 
     lane = lax.broadcasted_iota(jnp.int32, (rows, head_dim), 1)
     row_id = lax.broadcasted_iota(jnp.int32, (rows, head_dim), 0)
@@ -313,13 +332,6 @@
         return carry
 
     lax.fori_loop(0, HEADS, ext_body, 0)
-
-    def gather_step(stage):
-        for copy in gather_copies(stage - 1):
-            copy.wait_recv()
-        if stage <= STAGES:
-            for copy in gather_copies(stage):
-                copy.start()
 
     n_slot = HEADS * n_cand
     slot_lane = lax.broadcasted_iota(jnp.int32, (n_slot, head_dim), 1)
@@ -368,77 +380,53 @@
         for a, i in enumerate(slots):
             part[i] = acc[a * n_slot : (a + 1) * n_slot]
 
-    stage_slots = [(2 * k, 2 * k + 1, 8 + 2 * k, 9 + 2 * k) for k in range(STAGES)]
-    stage_slots[0] += (OWN,)
-    stage_slots[STAGES - 1] = stage_slots[STAGES - 1][:-1]
-
-    def rs_copy(i, step):
-        return remote(rs_s.at[i], rs_r.at[i], rs_ss.at[i], rs_rs.at[i], along(step))
-
-    def odd_sends(stage):
-        k = STAGES - stage
-        rs_s[4 + k] = part[2 * stage - 2].astype(BF16)
-        rs_copy(4 + k, -1).start()
-        rs_s[12 + k] = part[6 + 2 * stage].astype(BF16)
-        rs_copy(12 + k, 1).start()
-
-    gather_step(2)
-    qn_sends(0)
+    def rs_copy(i):
+        return remote(rs_s.at[i], rs_r.at[i], rs_ss.at[i], rs_rs.at[i], along(-HOPS[i][1]))
+
+    def sum_start(*slots):
+        for i in slots:
+            rs_s[i] = part[i].astype(BF16)
+            rs_copy(i).start()
+
+    def arrived(*slots):
+        for i in slots:
+            rs_copy(i).wait_recv()
+        return sum(rs_r[i].astype(F32) for i in slots)
+
+    def relay(i, *slots):
+        rs_s[i] = (part[i] + arrived(*slots)).astype(BF16)
+        rs_copy(i).start()
+
     for b in range(blocks):
         w_copy(0, b).wait()
         u = silu(jnp.dot(nv[...], w[b], preferred_element_type=F32))
         uv[:, b * bw : (b + 1) * bw] = u.astype(BF16)
-    name_users(stage_slots[0])
-    gather_step(3)
+    gather_wait(2, 10)
+    gather_start(3, 1, 11, 9)
     qn_sends(2)
+    gather_wait(5, 13)
+    gather_start(7, 6, 4, 14, 12)
+    qn_sends(4)
+    gather_wait(0, 8)
+    first = (OWN, 0, 8, 2, 10)
+    second = (5, 13, 1, 3, 9, 11)
+    last = (4, 6, 7, 12, 14)
+    name_users(first)
     kv_wait(near)
-    score(stage_slots[0], near, True)
-    name_users(stage_slots[1])
-    score(stage_slots[1], near, True)
-    gather_step(4)
-    qn_sends(4)
+    score(first, near, True)
+    gather_wait(3, 1, 11, 9)
+    qn_sends(6)
+    name_users(second)
+    score(second, near, True)
+    gather_wait(7, 6, 4, 14, 12)
+    name_users(last)
     kv_wait(far)
-    score(stage_slots[0], far, False)
-    odd_sends(1)
-    score(stage_slots[1], far, False)
-    odd_sends(2)
-    name_users(stage_slots[2])
-    score(stage_slots[2], near + far, True)
-    odd_sends(3)
-    qn_sends(6)
-    gather_step(5)
-    name_users(stage_slots[3])
-    score(stage_slots[3], near + far, True)
-    odd_sends(4)
-
-    def arrived(stage):
-        k = stage - 1
-        low = rs_r[k].astype(F32) + rs_r[4 + k].astype(F32)
-        high = rs_r[12 + k].astype(F32)
-        if stage > 1:
-            high = high + rs_r[8 + k].astype(F32)
-        return low, high
-
-    def rs_wait(stage):
-        k = stage - 1
-        rs_copy(k, -2).wait_recv()
-        rs_copy(4 + k, -1).wait_recv()
-        if stage > 1:
-            rs_copy(8 + k, 2).wait_recv()
-        rs_copy(12 + k, 1).wait_recv()
-
-    def rs_step(stage):
-        k = stage - 1
-        e = 2 * WIN // 2 + 2 - 2 * stage
-        if stage == 1:
-            rs_s[k] = part[e - 1].astype(BF16)
-        else:
-            rs_wait(stage - 1)
-            low, high = arrived(stage - 1)
-            rs_s[k] = (part[e - 1] + low).astype(BF16)
-            rs_s[8 + k] = (part[7 + e] + high).astype(BF16)
-            rs_copy(8 + k, 2).start()
-        rs_copy(k, -2).start()
+    score(last, near + far, True)
+    sum_start(*last)
+    score(second, far, False)
+    sum_start(1, 3, 9, 11)
+    score(first, far, False)
+    sum_start(0, 8)
 
     one_row = lax.broadcasted_iota(jnp.int32, (rows, rows), 0)
     one_col = lax.broadcasted_iota(jnp.int32, (rows, rows), 1)
@@ -509,26 +497,24 @@
             an_s[2 * p + 1] = more[rows:].astype(BF16)
         an_s[2 * p] = acc.astype(BF16)
 
-    rs_step(1)
-    attend_own(0)
-    attend_own(1)
-    attend_own(2)
-    rs_step(2)
     attend_next(0)
     an_copy(0).start()
     an_copy(1).start()
     attend_next(1)
+    relay(5, 4, 6, 7)
+    relay(13, 12, 14)
     an_copy(2).start()
+    an_copy(3).start()
+    relay(2, 1, 3)
+    relay(10, 9, 11)
     attend_next(2)
     attend_next(3)
-    rs_step(3)
-    an_copy(3).start()
     an_copy(4).start()
     an_copy(5).start()
-    attend_own(3)
+    an_copy(6).start()
+    for p in range(HEADS // 2):
+        attend_own(p)
     at_r[r] = at_s[r]
-    rs_step(4)
-    an_copy(6).start()
     u_c = jnp.concatenate(
         [
             silu(jnp.dot(cnormed, w[b], preferred_element_type=F32)).astype(BF16)
@@ -537,9 +523,8 @@
         axis=1,
     ).astype(F32)
 
-    rs_wait(4)
-    low, high = arrived(4)
-    cat_s[...] = (part[OWN] + low + high).reshape(HEADS, n_cand, head_dim)
+    sums = part[OWN] + arrived(0, 8, 2, 10, 5, 13)
+    cat_s[...] = sums.reshape(HEADS, n_cand, head_dim)
 
     def cat_copy(d):
         h = lax.rem(r + d, HEADS)
@@ -599,15 +584,10 @@
         qc_copy(d).wait_send()
         us_copy(d).wait_send()
         cat_copy(d).wait_send()
-    for stage in range(1, STAGES + 1):
-        for copy in gather_copies(stage):
-            copy.wait_send()
-        k = stage - 1
-        rs_copy(k, -2).wait_send()
-        rs_copy(4 + k, -1).wait_send()
-        if stage > 1:
-            rs_copy(8 + k, 2).wait_send()
-        rs_copy(12 + k, 1).wait_send()
+    for copy in gather_copies(HOPS):
+        copy.wait_send()
+    for i in HOPS:
+        rs_copy(i).wait_send()
 
     def drain(i, carry):
         h = lax.rem(r + i + 1, HEADS)

time: 83.9 us -> 81.7 us (0.974)
  the two profiles are of different devices: /device:TPU:40 before, /device:TPU:38 now
where the time goes in v4:
time: 81.7 us; the launch traced here: 81.6 us
  Pallas kernels  79.6 us (97%)
  local copies, waits for them, and re-layouts  1.41 us (2%)
    pallas_call x1, Pallas kernels, per_device(): pl.pallas_call(functools.partial(kernel, nz), out_shape=(pltpu.VMEM(histo...  79.6 us

profile of v4, /device:TPU:38, one launch (start us, length us, event | category | flops | bytes accessed | tf_op | source)
XLA Modules:
  0.0 81.6 jit_solution(5856919581743751237)
XLA Ops:
  0.6 79.6 %shard_map.77 = (bf16[256,1024]{1,0:T(8,128)(2,1)S(1)}, bf16[16,1024]{1,0:T(8,128)(2,1)S(1)}) custom-call(s32[4]{0:T(128)} %lens_in.1, s32[16]{0:T(128)} %users_in.1, bf16[16,1024]{1,0:T(8,128)(2,1)} %cand_in.1, bf16[256,1024]{1,0:T(8,128)(2,1)} %hist.1, bf16[1,1024,4096]{2,1,0:T(8,128)(2,1)} %w_in.1, bf16[1,1024,1024]{2,1,0:T(8,128)(2,1)} %w_out.1), custom_call_target="tpu_custom_call" | custom-call | tf_op jit(solution)/shard_map/pallas_call | solution.py:675
  80.2 0.8 copy.10
  81.0 0.6 copy.11

commit v5 on v4

--- a/solution.py
+++ b/solution.py
@@ -176,11 +176,6 @@
         for h in range(HEADS):
             pl.semaphore_signal(barrier, inc=1, device_id=in_rows(step, h), device_id_type=MESH)
 
-    pl.semaphore_wait(barrier, HEADS - 1 + 6 + 2 * HEADS)
-    for i in range(blocks):
-        w_copy(3, block_at(i)).start()
-        w_copy(1, block_at(i)).start()
-
     scale = 0.5 * head_dim ** (-0.5)
     for copy in small:
         copy.wait()
@@ -188,6 +183,10 @@
     per = bw // head_dim
     for b in range(blocks):
         w_copy(2, b).wait()
+        if b == 0:
+            for i in range(blocks):
+                w_copy(3, block_at(i)).start()
+                w_copy(1, block_at(i)).start()
         qc = silu(jnp.dot(cnormed, w[2 * blocks + b], preferred_element_type=F32)) * scale
         for i in range(per):
             qc_s[b * per + i] = qc[:, i * head_dim : (i + 1) * head_dim].astype(BF16)
@@ -217,6 +216,7 @@
         j = lax.rem(r - d + HEADS, HEADS)
         return remote(us_s.at[0], usr.at[OWN, j], us_ss.at[d], us_rs.at[d], in_row(j))
 
+    pl.semaphore_wait(barrier, HEADS - 1 + 6 + 2 * HEADS)
     for d in range(1, HEADS):
         qc_copy(d).start()
         us_copy(d).start()

time: 81.7 us -> 80.3 us (0.983)
  the two profiles are of different devices: /device:TPU:38 before, /device:TPU:46 now
where the time goes in v5:
time: 80.3 us; the launch traced here: 80.2 us
  Pallas kernels  78.2 us (97%)
  local copies, waits for them, and re-layouts  1.41 us (2%)
    pallas_call x1, Pallas kernels, per_device(): pl.pallas_call(functools.partial(kernel, nz), out_shape=(pltpu.VMEM(histo...  78.2 us

profile of v5, /device:TPU:46, one launch (start us, length us, event | category | flops | bytes accessed | tf_op | source)
XLA Modules:
  0.0 80.2 jit_solution(2272736715542304604)
XLA Ops:
  0.6 78.2 %shard_map.77 = (bf16[256,1024]{1,0:T(8,128)(2,1)S(1)}, bf16[16,1024]{1,0:T(8,128)(2,1)S(1)}) custom-call(s32[4]{0:T(128)} %lens_in.1, s32[16]{0:T(128)} %users_in.1, bf16[16,1024]{1,0:T(8,128)(2,1)} %cand_in.1, bf16[256,1024]{1,0:T(8,128)(2,1)} %hist.1, bf16[1,1024,4096]{2,1,0:T(8,128)(2,1)} %w_in.1, bf16[1,1024,1024]{2,1,0:T(8,128)(2,1)} %w_out.1), custom_call_target="tpu_custom_call" | custom-call | tf_op jit(solution)/shard_map/pallas_call | solution.py:675
  78.8 0.8 copy.10
  79.6 0.6 copy.11
